TPU v7x, 8 devices: a whole 2x2x1 slice. The times are simulated.
8 devices in a mesh: rep: 1 (over z), row: 2 (over y), col: 2 (over x), core: 2 (over core).
Axes of the slice: x: 2, y: 2, z: 1, core: 2. Of those that a mesh axis runs over, the one named last changes fastest.
Arguments:
- x: bfloat16 [2, 512, 640], P(None, ('rep', 'row', 'col', 'core'))
- route_idx: int32 [2, 512, 4], P(None, ('rep', 'row', 'col', 'core'))
- gates: float32 [2, 512, 4], P(None, ('rep', 'row', 'col', 'core'))
- w_gate: bfloat16 [128, 640, 640], P(('rep', 'row', 'col', 'core'))
- w_up: bfloat16 [128, 640, 640], P(('rep', 'row', 'col', 'core'))
- w_down: bfloat16 [128, 640, 640], P(('rep', 'row', 'col', 'core'))
- grad_y: bfloat16 [2, 512, 640], P(None, ('rep', 'row', 'col', 'core'))
Outputs:
- output 1: bfloat16 [2, 512, 640], P(None, ('rep', 'row', 'col', 'core'))
- output 2: bfloat16 [2, 512, 640], P(None, ('rep', 'row', 'col', 'core'))
- output 3: float32 [2, 512, 4], P(None, ('rep', 'row', 'col', 'core'))
- output 4: float32 [128, 640, 640], P(('rep', 'row', 'col', 'core'))
- output 5: float32 [128, 640, 640], P(('rep', 'row', 'col', 'core'))
- output 6: float32 [128, 640, 640], P(('rep', 'row', 'col', 'core'))
All inputs are finite; a program needn't handle non-finite values.
Results may differ from a plain program's by a relative error of at most 0.00854886.
Values are sent between devices in bfloat16 or wider.
A program may use at most 1 GiB of HBM per device.

v0:
```python
import jax
import jax.numpy as jnp
from jax import lax
from jax.sharding import PartitionSpec as P

GROUP_AXES = ("row", "col", "core")
ALL_AXES = ("rep", "row", "col", "core")


def route_tables(route_ids, gates, group_size, capacity, local_experts):
    expert_ids = jnp.arange(group_size)[None, :] * local_experts + jnp.arange(local_experts)[:, None]
    expert_hits = route_ids[None, None, :, :] == expert_ids[:, :, None, None]
    member = jnp.sum(expert_hits.astype(jnp.int32), axis=3)
    slot_rank = jnp.cumsum(member, axis=2) - member
    disp_mask = (member[:, :, None, :] > 0) & (slot_rank[:, :, None, :] == jnp.arange(capacity)[None, None, :, None])
    slot_pos = jnp.sum(jnp.where(expert_hits, slot_rank[:, :, :, None], 0), axis=(0, 1))
    slot_addr = (route_ids % local_experts) * (group_size * capacity) + (route_ids // local_experts) * capacity + slot_pos
    row_gate = jnp.zeros((local_experts * group_size * capacity,), jnp.float32).at[slot_addr.reshape(-1)].set(gates.reshape(-1))
    return disp_mask.astype(jnp.bfloat16), slot_addr, row_gate


def expert_forward(x_rows, w_gate, w_up, w_down):
    gate_pre = jnp.einsum("lnd,ldf->lnf", x_rows, w_gate, preferred_element_type=jnp.float32).astype(jnp.bfloat16)
    up_pre = jnp.einsum("lnd,ldf->lnf", x_rows, w_up, preferred_element_type=jnp.float32).astype(jnp.bfloat16)
    gate_f = gate_pre.astype(jnp.float32)
    hidden = (gate_f * jax.nn.sigmoid(gate_f) * up_pre.astype(jnp.float32)).astype(jnp.bfloat16)
    exp_out = jnp.einsum("lnf,lfd->lnd", hidden, w_down, preferred_element_type=jnp.float32).astype(jnp.bfloat16)
    return exp_out, gate_pre, up_pre, hidden


def expert_backward(x_rows, d_out, gate_pre, up_pre, hidden, w_gate, w_up, w_down):
    gate_f = gate_pre.astype(jnp.float32)
    up_f = up_pre.astype(jnp.float32)
    sigmoid_g = jax.nn.sigmoid(gate_f)
    d_act = jnp.einsum("lnd,lfd->lnf", d_out, w_down, preferred_element_type=jnp.float32)
    d_up = (d_act * gate_f * sigmoid_g).astype(jnp.bfloat16)
    d_gate = (d_act * up_f * sigmoid_g * (1.0 + gate_f * (1.0 - sigmoid_g))).astype(jnp.bfloat16)
    g_down = jnp.einsum("lnf,lnd->lfd", hidden, d_out, preferred_element_type=jnp.float32)
    g_gate = jnp.einsum("lnd,lnf->ldf", x_rows, d_gate, preferred_element_type=jnp.float32)
    g_up = jnp.einsum("lnd,lnf->ldf", x_rows, d_up, preferred_element_type=jnp.float32)
    d_in = (jnp.einsum("lnf,ldf->lnd", d_gate, w_gate, preferred_element_type=jnp.float32) + jnp.einsum("lnf,ldf->lnd", d_up, w_up, preferred_element_type=jnp.float32)).astype(jnp.bfloat16)
    return d_in, g_gate, g_up, g_down


def solution(mesh):
    group_size = mesh.shape["row"] * mesh.shape["col"] * mesh.shape["core"]
    tok_spec = P(None, ALL_AXES, None)
    w_spec = P(ALL_AXES, None, None)

    def exchange(send_buf):
        return lax.all_to_all(send_buf, GROUP_AXES, 1, 1, tiled=True)

    def moe_layer(x, route_idx, gates, w_gate, w_up, w_down, grad_y):
        local_experts = w_gate.shape[0]
        tok_dev = x.shape[1]
        model_dim = x.shape[2]
        capacity = tok_dev // 2
        buf_rows = group_size * capacity
        buf_shape = (local_experts, group_size, capacity, model_dim)
        flat_shape = (local_experts * buf_rows, model_dim)
        outs_y, outs_dx, outs_dg = [], [], []
        sum_gate = jnp.zeros(w_gate.shape, jnp.float32)
        sum_up = jnp.zeros(w_up.shape, jnp.float32)
        sum_down = jnp.zeros(w_down.shape, jnp.float32)
        for micro_idx in range(2):
            x_mb = x[micro_idx]
            dy_mb = grad_y[micro_idx]
            gate_mb = gates[micro_idx]
            disp_mask, slot_addr, row_gate = route_tables(route_idx[micro_idx], gate_mb, group_size, capacity, local_experts)
            send_x = jnp.einsum("lgct,td->lgcd", disp_mask, x_mb, preferred_element_type=jnp.float32).astype(jnp.bfloat16)
            x_rows = exchange(send_x).reshape(local_experts, buf_rows, model_dim)
            exp_out, gate_pre, up_pre, hidden = expert_forward(x_rows, w_gate, w_up, w_down)
            out_back = exchange(exp_out.reshape(buf_shape)).reshape(flat_shape)
            out_slots = jnp.take(out_back, slot_addr, axis=0)
            outs_y.append(jnp.sum(gate_mb[:, :, None] * out_slots.astype(jnp.float32), axis=1).astype(jnp.bfloat16))
            outs_dg.append(jnp.einsum("td,tkd->tk", dy_mb, out_slots, preferred_element_type=jnp.float32))
            dy_rows = jnp.einsum("lgct,td->lgcd", disp_mask, dy_mb, preferred_element_type=jnp.float32)
            send_dout = (row_gate.reshape(local_experts, group_size, capacity)[..., None] * dy_rows).astype(jnp.bfloat16)
            d_out = exchange(send_dout).reshape(local_experts, buf_rows, model_dim)
            d_in, g_gate, g_up, g_down = expert_backward(x_rows, d_out, gate_pre, up_pre, hidden, w_gate, w_up, w_down)
            dx_back = exchange(d_in.reshape(buf_shape)).reshape(flat_shape)
            outs_dx.append(jnp.sum(jnp.take(dx_back, slot_addr, axis=0).astype(jnp.float32), axis=1).astype(jnp.bfloat16))
            sum_gate = sum_gate + g_gate
            sum_up = sum_up + g_up
            sum_down = sum_down + g_down
        return (jnp.stack(outs_y), jnp.stack(outs_dx), jnp.stack(outs_dg), sum_gate, sum_up, sum_down)

    return jax.shard_map(moe_layer, mesh=mesh, in_specs=(tok_spec, tok_spec, tok_spec, w_spec, w_spec, w_spec, tok_spec), out_specs=(tok_spec, tok_spec, tok_spec, w_spec, w_spec, w_spec), check_vma=False)
```

profile of v0, /device:TPU:0, one launch (start us, length us, event | category | flops | bytes accessed | tf_op | source)
XLA Modules:
  0.0 598.4 jit_solution(12926214734038831180)
XLA Ops:
  1.5 3.5 reduce_window_sum.17
  5.2 3.5 reduce_window_sum.18
  14.1 4.3 all-to-all-start.2
  35.6 43.2 %all-to-all-done.2 = bf16[16,8,32,640]{3,2,0,1:T(8,128)(2,1)} async-done(((bf16[16,8,32,640]{3,2,0,1:T(8,128)(2,1)}), bf16[16,8,32,640]{3,2,0,1:T(8,128)(2,1)}, u32[]{:S(2)}, u32[]{:S(2)}) %all-to-all-start.2) | async-done | bytes 5242912 | tf_op jit(solution)/shard_map/all_to_all | solution.py:51
  78.8 3.9 all-to-all-start.6
  92.5 14.4 %convolution_convert_fusion.4 = bf16[16,256,640]{2,1,0:T(8,128)(2,1)} fusion(bf16[16,256,640]{2,1,0:T(8,128)(2,1)S(1)} %bitcast.100, bf16[16,640,640]{2,1,0:T(8,128)(2,1)} %param.12), kind=kOutput, calls=%fused_computation.49 | convolution fusion | flops 3358064640 | bytes 23592960 | tf_op jit(solution)/shard_map/lnd,ldf->lnf/dot_general | solution.py:23
  106.9 6.5 %convolution_convert_fusion.3 = bf16[16,256,640]{2,1,0:T(8,128)(2,1)} fusion(bf16[16,256,640]{2,1,0:T(8,128)(2,1)S(1)} %bitcast.101, bf16[16,640,640]{2,1,0:T(8,128)(2,1)S(1)} %bitcast.111), kind=kOutput, calls=%fused_computation.48 | convolution fusion | flops 3358064640 | bytes 23592960 | tf_op jit(solution)/shard_map/lnd,ldf->lnf/dot_general | solution.py:24
  113.4 29.5 %all-to-all-done.6 = bf16[16,8,32,640]{3,2,0,1:T(8,128)(2,1)} async-done(((bf16[16,8,32,640]{3,2,0,1:T(8,128)(2,1)}), bf16[16,8,32,640]{3,2,0,1:T(8,128)(2,1)}, u32[]{:S(2)}, u32[]{:S(2)}) %all-to-all-start.6) | async-done | bytes 5242912 | tf_op jit(solution)/shard_map/all_to_all | solution.py:51
  143.0 3.6 all-to-all-start
  146.5 15.2 %convolution_convert_fusion.2 = bf16[16,256,640]{2,1,0:T(8,128)(2,1)} fusion(bf16[16,640,640]{2,1,0:T(8,128)(2,1)} %param.14, bf16[16,256,640]{2,1,0:T(8,128)(2,1)} %convolution_convert_fusion.3, bf16[16,256,640]{2,1,0:T(8,128)(2,1)} %convolution_convert_fusion.4), kind=kOutput, calls=%fused_computation.47 | convolution fusion | flops 3379036160 | bytes 28835840 | tf_op jit(solution)/shard_map/lnf,lfd->lnd/dot_general | solution.py:27
  161.7 5.6 copy.119
  167.3 15.7 %fusion.7 = (bf16[16,256,640]{2,1,0:T(8,128)(2,1)}, f32[16,256,640]{2,1,0:T(8,128)}) fusion(bf16[16,256,640]{2,1,0:T(8,128)(2,1)} %convolution_convert_fusion.3, bf16[16,256,640]{2,1,0:T(8,128)(2,1)} %convolution_convert_fusion.4, bf16[16,256,640]{2,1,0:T(8,128)(2,1)} %bitcast.120, bf16[16,640,640]{2,1,0:T(8,128)(2,1)} %param.14), kind=kOutput, calls=%fused_computation.28 | convolution fusion | flops 3386900480 | bytes 44564480 | tf_op jit(solution)/shard_map/lnd,lfd->lnf/dot_general | solution.py:35
  183.0 23.8 %all-to-all-done = bf16[16,8,32,640]{3,2,0,1:T(8,128)(2,1)} async-done(((bf16[16,8,32,640]{3,2,0,1:T(8,128)(2,1)}), bf16[16,8,32,640]{3,2,0,1:T(8,128)(2,1)}, u32[]{:S(2)}, u32[]{:S(2)}) %all-to-all-start) | async-done | bytes 5242912 | tf_op jit(solution)/shard_map/all_to_all | solution.py:51
  206.8 3.6 all-to-all-start.4
  210.4 3.3 copy.94
  213.8 13.7 %convolution_convert_fusion.7 = bf16[16,256,640]{2,1,0:T(8,128)(2,1)} fusion(bf16[16,256,640]{2,1,0:T(8,128)(2,1)S(1)} %bitcast.106, bf16[16,640,640]{2,1,0:T(8,128)(2,1)} %param.12), kind=kOutput, calls=%fused_computation.52 | convolution fusion | flops 3358064640 | bytes 23592960 | tf_op jit(solution)/shard_map/lnd,ldf->lnf/dot_general | solution.py:23
  230.4 6.5 %convolution_convert_fusion.6 = bf16[16,256,640]{2,1,0:T(8,128)(2,1)} fusion(bf16[16,256,640]{2,1,0:T(8,128)(2,1)S(1)} %bitcast.107, bf16[16,640,640]{2,1,0:T(8,128)(2,1)S(1)} %bitcast.113), kind=kOutput, calls=%fused_computation.51 | convolution fusion | flops 3358064640 | bytes 23592960 | tf_op jit(solution)/shard_map/lnd,ldf->lnf/dot_general | solution.py:24
  236.9 15.9 %fusion.89 = f32[16,256,640]{2,1,0:T(8,128)} fusion(bf16[16,256,640]{2,1,0:T(8,128)(2,1)} %get-tuple-element.25, bf16[16,640,640]{2,1,0:T(8,128)(2,1)} %param.12), kind=kOutput, calls=%fused_computation.167 | convolution fusion | flops 3355443200 | bytes 28835840 | tf_op jit(solution)/shard_map/lnf,ldf->lnd/dot_general | solution.py:41
  252.7 17.9 %all-to-all-done.4 = bf16[16,8,32,640]{3,2,0,1:T(8,128)(2,1)} async-done(((bf16[16,8,32,640]{3,2,0,1:T(8,128)(2,1)}), bf16[16,8,32,640]{3,2,0,1:T(8,128)(2,1)}, u32[]{:S(2)}, u32[]{:S(2)}) %all-to-all-start.4) | async-done | bytes 5242912 | tf_op jit(solution)/shard_map/all_to_all | solution.py:51
  270.7 3.6 all-to-all-start.3
  274.3 5.7 copy.110
  279.9 18.1 %fusion.78 = f32[16,640,640]{2,1,0:T(8,128)} fusion(bf16[16,256,640]{2,1,0:T(8,128)(2,1)} %bitcast.126, bf16[16,256,640]{2,1,0:T(8,128)(2,1)} %convolution_convert_fusion.6, bf16[16,256,640]{2,1,0:T(8,128)(2,1)S(1)} %bitcast.119), kind=kOutput, calls=%fused_computation.162 | convolution fusion | flops 3376414720 | bytes 41943040 | tf_op jit(solution)/shard_map/lnf,lnd->lfd/dot_general | solution.py:38
  298.0 21.6 %convolution_add_fusion = f32[16,640,640]{2,1,0:T(8,128)} fusion(f32[16,640,640]{2,1,0:T(8,128)} %fusion.78, bf16[16,256,640]{2,1,0:T(8,128)(2,1)} %bitcast.121, bf16[16,256,640]{2,1,0:T(8,128)(2,1)} %convolution_convert_fusion.3, bf16[16,256,640]{2,1,0:T(8,128)(2,1)} %convolution_convert_fusion.4), kind=kOutput, calls=%fused_computation.18 | convolution fusion | flops 3382968320 | bytes 68157440 | tf_op jit(solution)/shard_map/lnf,lnd->lfd/dot_general | solution.py:38
  319.6 25.5 %add_convert_fusion = bf16[16,256,640]{2,1,0:T(8,128)(2,1)} fusion(f32[16,256,640]{2,1,0:T(8,128)} %fusion.89, bf16[16,640,640]{2,1,0:T(8,128)(2,1)} %param.13, f32[16,256,640]{2,1,0:T(8,128)} %get-tuple-element.26, bf16[16,256,640]{2,1,0:T(8,128)(2,1)} %convolution_convert_fusion.4), kind=kOutput, calls=%fused_computation.41 | convolution fusion | flops 3379036160 | bytes 44564480 | tf_op jit(solution)/shard_map/lnf,ldf->lnd/dot_general | solution.py:41
  345.1 15.2 %convolution_convert_fusion.5 = bf16[16,256,640]{2,1,0:T(8,128)(2,1)} fusion(bf16[16,640,640]{2,1,0:T(8,128)(2,1)} %param.14, bf16[16,256,640]{2,1,0:T(8,128)(2,1)} %convolution_convert_fusion.6, bf16[16,256,640]{2,1,0:T(8,128)(2,1)} %convolution_convert_fusion.7), kind=kOutput, calls=%fused_computation.50 | convolution fusion | flops 3379036160 | bytes 28835840 | tf_op jit(solution)/shard_map/lnf,lfd->lnd/dot_general | solution.py:27
  360.3 5.5 copy.95
  365.8 15.5 %fusion.3 = (bf16[16,256,640]{2,1,0:T(8,128)(2,1)}, f32[16,256,640]{2,1,0:T(8,128)}) fusion(bf16[16,256,640]{2,1,0:T(8,128)(2,1)} %convolution_convert_fusion.6, bf16[16,256,640]{2,1,0:T(8,128)(2,1)} %convolution_convert_fusion.7, bf16[16,256,640]{2,1,0:T(8,128)(2,1)} %bitcast.127, bf16[16,640,640]{2,1,0:T(8,128)(2,1)} %param.14), kind=kOutput, calls=%fused_computation.24 | convolution fusion | flops 3386900480 | bytes 44564480 | tf_op jit(solution)/shard_map/lnd,lfd->lnf/dot_general | solution.py:35
  381.3 3.6 all-to-all-start.1
  384.9 15.9 %fusion.88 = f32[16,256,640]{2,1,0:T(8,128)} fusion(bf16[16,256,640]{2,1,0:T(8,128)(2,1)} %get-tuple-element.27, bf16[16,640,640]{2,1,0:T(8,128)(2,1)} %param.12), kind=kOutput, calls=%fused_computation.166 | convolution fusion | flops 3355443200 | bytes 28835840 | tf_op jit(solution)/shard_map/lnf,ldf->lnd/dot_general | solution.py:41
  400.7 5.4 copy.120
  406.1 25.0 %add_convert_fusion.1 = bf16[16,256,640]{2,1,0:T(8,128)(2,1)} fusion(f32[16,256,640]{2,1,0:T(8,128)} %fusion.88, bf16[16,640,640]{2,1,0:T(8,128)(2,1)} %param.13, f32[16,256,640]{2,1,0:T(8,128)} %get-tuple-element.28, bf16[16,256,640]{2,1,0:T(8,128)(2,1)} %convolution_convert_fusion.7), kind=kOutput, calls=%fused_computation.43 | convolution fusion | flops 3379036160 | bytes 44564480 | tf_op jit(solution)/shard_map/lnf,ldf->lnd/dot_general | solution.py:41
  431.2 13.9 %all-to-all-done.1 = bf16[16,8,32,640]{3,2,0,1:T(8,128)(2,1)} async-done(((bf16[16,8,32,640]{3,2,0,1:T(8,128)(2,1)}), bf16[16,8,32,640]{3,2,0,1:T(8,128)(2,1)}, u32[]{:S(2)}, u32[]{:S(2)}) %all-to-all-start.1) | async-done | bytes 5242912 | tf_op jit(solution)/shard_map/all_to_all | solution.py:51
  445.1 3.4 all-to-all-start.7
  448.5 15.7 %fusion.83 = f32[16,640,640]{2,1,0:T(8,128)} fusion(bf16[16,256,640]{2,1,0:T(8,128)(2,1)} %bitcast.108, f32[16,256,640]{2,1,0:T(8,128)} %get-tuple-element.28, bf16[16,256,640]{2,1,0:T(8,128)(2,1)} %convolution_convert_fusion.7), kind=kOutput, calls=%fused_computation.163 | convolution fusion | flops 3373793280 | bytes 47185920 | tf_op jit(solution)/shard_map/lnd,lnf->ldf/dot_general | solution.py:40
  464.2 5.6 copy.111
  469.8 23.3 %convolution_add_fusion.1 = f32[16,640,640]{2,1,0:T(8,128)} fusion(f32[16,640,640]{2,1,0:T(8,128)} %fusion.83, bf16[16,256,640]{2,1,0:T(8,128)(2,1)S(1)} %bitcast.105, f32[16,256,640]{2,1,0:T(8,128)} %get-tuple-element.26, bf16[16,256,640]{2,1,0:T(8,128)(2,1)} %convolution_convert_fusion.4), kind=kOutput, calls=%fused_computation.19 | convolution fusion | flops 3380346880 | bytes 73400320 | tf_op jit(solution)/shard_map/lnd,lnf->ldf/dot_general | solution.py:40
  493.1 15.6 %all-to-all-done.7 = bf16[16,8,32,640]{3,2,0,1:T(8,128)(2,1)} async-done(((bf16[16,8,32,640]{3,2,0,1:T(8,128)(2,1)}), bf16[16,8,32,640]{3,2,0,1:T(8,128)(2,1)}, u32[]{:S(2)}, u32[]{:S(2)}) %all-to-all-start.7) | async-done | bytes 5242912 | tf_op jit(solution)/shard_map/all_to_all | solution.py:51
  508.8 3.6 all-to-all-start.5
  512.4 17.6 %fusion.90 = f32[16,640,640]{2,1,0:T(8,128)} fusion(bf16[16,256,640]{2,1,0:T(8,128)(2,1)} %bitcast.109, bf16[16,256,640]{2,1,0:T(8,128)(2,1)} %get-tuple-element.27), kind=kOutput, calls=%fused_computation.168 | convolution fusion | flops 3355443200 | bytes 36700160 | tf_op jit(solution)/shard_map/lnd,lnf->ldf/dot_general | solution.py:39
  530.0 21.9 %convolution_add_fusion.2 = f32[16,640,640]{2,1,0:T(8,128)} fusion(f32[16,640,640]{2,1,0:T(8,128)} %fusion.90, bf16[16,256,640]{2,1,0:T(8,128)(2,1)} %bitcast.102, bf16[16,256,640]{2,1,0:T(8,128)(2,1)} %get-tuple-element.25), kind=kOutput, calls=%fused_computation.20 | convolution fusion | flops 3361996800 | bytes 62914560 | tf_op jit(solution)/shard_map/lnd,lnf->ldf/dot_general | solution.py:39
  551.9 5.6 copy.103
  557.5 4.5 gather_fusion.1
  562.8 5.6 copy.96
  568.4 4.5 gather_fusion
  573.7 5.6 copy.121
  579.3 4.5 gather_fusion.3
  585.5 5.6 copy.112
  591.0 4.5 gather_fusion.2
  (129 shorter events, 41.9 us)
Async XLA Ops:
  11.1 7.5 %copy-start.13 = (f32[2,64,4]{1,2,0:T(4,128)S(1)}, f32[2,64,4]{1,2,0:T(4,128)}, u32[]{:S(2)}) copy-start(f32[2,64,4]{1,2,0:T(4,128)} %param.11) | copy-start | bytes 6148
  11.1 11.5 %copy-start.12 = (s32[2,64,4]{1,2,0:T(4,128)S(1)}, s32[2,64,4]{1,2,0:T(4,128)}, u32[]{:S(2)}) copy-start(s32[2,64,4]{1,2,0:T(4,128)} %param.10) | copy-start | bytes 6148
  11.1 15.0 %copy-start.4 = (bf16[2,64,640]{2,1,0:T(8,128)(2,1)S(1)}, bf16[2,64,640]{2,1,0:T(8,128)(2,1)}, u32[]{:S(2)}) copy-start(bf16[2,64,640]{2,1,0:T(8,128)(2,1)} %param.15) | copy-start | bytes 491524
  14.1 64.7 %all-to-all-start.2 = ((bf16[16,8,32,640]{3,2,0,1:T(8,128)(2,1)}), bf16[16,8,32,640]{3,2,0,1:T(8,128)(2,1)}, u32[]{:S(2)}, u32[]{:S(2)}) async-start(bf16[16,8,32,640]{3,2,0,1:T(8,128)(2,1)} %copy.100), calls=%async_computation.2 | async-start | bytes 10485760 | tf_op jit(solution)/shard_map/all_to_all | solution.py:51
  32.6 50.1 %copy-start.5 = (bf16[2,64,640]{2,1,0:T(8,128)(2,1)S(1)}, bf16[2,64,640]{2,1,0:T(8,128)(2,1)}, u32[]{:S(2)}) copy-start(bf16[2,64,640]{2,1,0:T(8,128)(2,1)} %param.9) | copy-start | bytes 491524
  78.8 64.1 %all-to-all-start.6 = ((bf16[16,8,32,640]{3,2,0,1:T(8,128)(2,1)}), bf16[16,8,32,640]{3,2,0,1:T(8,128)(2,1)}, u32[]{:S(2)}, u32[]{:S(2)}) async-start(bf16[16,8,32,640]{3,2,0,1:T(8,128)(2,1)} %copy.118), calls=%async_computation.6 | async-start | bytes 10485760 | tf_op jit(solution)/shard_map/all_to_all | solution.py:51
  89.1 17.8 %slice-start.2 = ((s8[13107200]{0:T(1024)(128)(4,1)}), s8[4194304]{0:T(1024)(128)(4,1)S(1)}, s32[]{:S(2)}) async-start(s8[13107200]{0:T(1024)(128)(4,1)} %bitcast.110), calls=%async_computation.10 | async-start | bytes 8388608
  89.1 17.8 %slice-start.3 = ((s8[13107200]{0:T(1024)(128)(4,1)}), s8[4194304]{0:T(1024)(128)(4,1)S(1)}, s32[]{:S(2)}) async-start(s8[13107200]{0:T(1024)(128)(4,1)} %bitcast.110), calls=%async_computation.11 | async-start | bytes 8388608
  92.4 14.4 %copy-start = (bf16[16,8,32,640]{3,2,1,0:T(8,128)(2,1)}, bf16[16,8,32,640]{3,2,1,0:T(8,128)(2,1)S(1)}, u32[]{:S(2)}) copy-start(bf16[16,8,32,640]{3,2,1,0:T(8,128)(2,1)S(1)} %copy.101) | copy-start | bytes 15728644
  92.4 14.4 %slice-start.4 = ((s8[13107200]{0:T(1024)(128)(4,1)}), s8[4194304]{0:T(1024)(128)(4,1)S(1)}, s32[]{:S(2)}) async-start(s8[13107200]{0:T(1024)(128)(4,1)} %bitcast.110), calls=%async_computation.12 | async-start | bytes 8388608
  92.5 14.4 %slice-start.5 = ((s8[13107200]{0:T(1024)(128)(4,1)}), s8[524288]{0:T(1024)(128)(4,1)S(1)}, s32[]{:S(2)}) async-start(s8[13107200]{0:T(1024)(128)(4,1)} %bitcast.110), calls=%async_computation.13 | async-start | bytes 1048576
  143.0 63.8 %all-to-all-start = ((bf16[16,8,32,640]{3,2,0,1:T(8,128)(2,1)}), bf16[16,8,32,640]{3,2,0,1:T(8,128)(2,1)}, u32[]{:S(2)}, u32[]{:S(2)}) async-start(bf16[16,8,32,640]{3,2,0,1:T(8,128)(2,1)} %copy.93), calls=%async_computation | async-start | bytes 10485760 | tf_op jit(solution)/shard_map/all_to_all | solution.py:51
  206.8 63.9 %all-to-all-start.4 = ((bf16[16,8,32,640]{3,2,0,1:T(8,128)(2,1)}), bf16[16,8,32,640]{3,2,0,1:T(8,128)(2,1)}, u32[]{:S(2)}, u32[]{:S(2)}) async-start(bf16[16,8,32,640]{3,2,0,1:T(8,128)(2,1)} %copy.109), calls=%async_computation.4 | async-start | bytes 10485760 | tf_op jit(solution)/shard_map/all_to_all | solution.py:51
  210.4 17.1 %slice-start.12 = ((s8[5242880]{0:T(1024)(128)(4,1)}), s8[4194304]{0:T(1024)(128)(4,1)S(1)}, s32[]{:S(2)}) async-start(s8[5242880]{0:T(1024)(128)(4,1)} %bitcast.123), calls=%async_computation.20 | async-start | bytes 8388608
  213.7 16.6 %copy-start.1 = (bf16[16,8,32,640]{3,2,1,0:T(8,128)(2,1)}, bf16[16,8,32,640]{3,2,1,0:T(8,128)(2,1)S(1)}, u32[]{:S(2)}) copy-start(bf16[16,8,32,640]{3,2,1,0:T(8,128)(2,1)S(1)} %copy.94) | copy-start | bytes 15728644
  213.7 13.7 %slice-start.13 = ((s8[5242880]{0:T(1024)(128)(4,1)}), s8[1048576]{0:T(1024)(128)(4,1)S(1)}, s32[]{:S(2)}) async-start(s8[5242880]{0:T(1024)(128)(4,1)} %bitcast.123), calls=%async_computation.21 | async-start | bytes 2097152
  213.8 16.6 %slice-start.6 = ((s8[13107200]{0:T(1024)(128)(4,1)}), s8[4194304]{0:T(1024)(128)(4,1)S(1)}, s32[]{:S(2)}) async-start(s8[13107200]{0:T(1024)(128)(4,1)} %bitcast.112), calls=%async_computation.14 | async-start | bytes 8388608
  213.8 16.6 %slice-start.7 = ((s8[13107200]{0:T(1024)(128)(4,1)}), s8[4194304]{0:T(1024)(128)(4,1)S(1)}, s32[]{:S(2)}) async-start(s8[13107200]{0:T(1024)(128)(4,1)} %bitcast.112), calls=%async_computation.15 | async-start | bytes 8388608
  213.8 16.6 %slice-start.8 = ((s8[13107200]{0:T(1024)(128)(4,1)}), s8[4194304]{0:T(1024)(128)(4,1)S(1)}, s32[]{:S(2)}) async-start(s8[13107200]{0:T(1024)(128)(4,1)} %bitcast.112), calls=%async_computation.16 | async-start | bytes 8388608
  227.5 2.9 slice-start.9
  252.7 27.2 %slice-start.10 = ((s8[5242880]{0:T(1024)(128)(4,1)}), s8[1048576]{0:T(1024)(128)(4,1)S(1)}, s32[]{:S(2)}) async-start(s8[5242880]{0:T(1024)(128)(4,1)} %bitcast.118), calls=%async_computation.18 | async-start | bytes 2097152
  270.7 110.6 %all-to-all-start.3 = ((bf16[16,8,32,640]{3,2,0,1:T(8,128)(2,1)}), bf16[16,8,32,640]{3,2,0,1:T(8,128)(2,1)}, u32[]{:S(2)}, u32[]{:S(2)}) async-start(bf16[16,8,32,640]{3,2,0,1:T(8,128)(2,1)} %copy.102), calls=%async_computation.3 | async-start | bytes 10485760 | tf_op jit(solution)/shard_map/all_to_all | solution.py:51
  274.3 5.7 slice-start.11
  381.3 63.9 %all-to-all-start.1 = ((bf16[16,8,32,640]{3,2,0,1:T(8,128)(2,1)}), bf16[16,8,32,640]{3,2,0,1:T(8,128)(2,1)}, u32[]{:S(2)}, u32[]{:S(2)}) async-start(bf16[16,8,32,640]{3,2,0,1:T(8,128)(2,1)} %copy.95), calls=%async_computation.1 | async-start | bytes 10485760 | tf_op jit(solution)/shard_map/all_to_all | solution.py:51
  445.1 63.6 %all-to-all-start.7 = ((bf16[16,8,32,640]{3,2,0,1:T(8,128)(2,1)}), bf16[16,8,32,640]{3,2,0,1:T(8,128)(2,1)}, u32[]{:S(2)}, u32[]{:S(2)}) async-start(bf16[16,8,32,640]{3,2,0,1:T(8,128)(2,1)} %copy.120), calls=%async_computation.7 | async-start | bytes 10485760 | tf_op jit(solution)/shard_map/all_to_all | solution.py:51
  464.2 5.6 slice-start
  464.2 5.6 slice-start.1
  508.8 76.7 %all-to-all-start.5 = ((bf16[16,8,32,640]{3,2,0,1:T(8,128)(2,1)}), bf16[16,8,32,640]{3,2,0,1:T(8,128)(2,1)}, u32[]{:S(2)}, u32[]{:S(2)}) async-start(bf16[16,8,32,640]{3,2,0,1:T(8,128)(2,1)} %copy.111), calls=%async_computation.5 | async-start | bytes 10485760 | tf_op jit(solution)/shard_map/all_to_all | solution.py:51
  551.9 5.6 copy-start.3
  551.9 10.2 %copy-start.9 = (bf16[64,640,1]{1,0,2:T(8,128)(2,1)S(1)}, bf16[64,640,1]{1,0,2:T(8,128)(2,1)}, u32[]{:S(2)}) copy-start(bf16[64,640,1]{1,0,2:T(8,128)(2,1)} %get-tuple-element.14) | copy-start | bytes 245764
  551.9 10.2 %copy-start.11 = (pred[64,4]{1,0:T(8,128)(4,1)S(1)}, pred[64,4]{1,0:T(8,128)(4,1)}, u32[]{:S(2)}) copy-start(pred[64,4]{1,0:T(8,128)(4,1)} %copy.99) | copy-start | bytes 772
  557.4 10.9 %copy-start.2 = (s32[1024]{0:T(1024)S(1)}, s32[1024]{0:T(1024)}, u32[]{:S(2)}) copy-start(s32[1024]{0:T(1024)} %pad_clamp_fusion.1) | copy-start | bytes 12292
  557.5 15.5 %copy-start.8 = (bf16[64,640,1]{1,0,2:T(8,128)(2,1)S(1)}, bf16[64,640,1]{1,0,2:T(8,128)(2,1)}, u32[]{:S(2)}) copy-start(bf16[64,640,1]{1,0,2:T(8,128)(2,1)} %get-tuple-element.13) | copy-start | bytes 245764
  557.5 15.5 %copy-start.10 = (pred[64,4]{1,0:T(8,128)(4,1)S(1)}, pred[64,4]{1,0:T(8,128)(4,1)}, u32[]{:S(2)}) copy-start(pred[64,4]{1,0:T(8,128)(4,1)} %copy.92) | copy-start | bytes 772
  568.4 15.9 %copy-start.7 = (f32[64,4]{1,0:T(8,128)S(1)}, f32[64,4]{1,0:T(8,128)}, u32[]{:S(2)}) copy-start(f32[64,4]{1,0:T(8,128)} %copy.98) | copy-start | bytes 3076
  568.4 16.5 %copy-start.6 = (f32[64,4]{1,0:T(8,128)S(1)}, f32[64,4]{1,0:T(8,128)}, u32[]{:S(2)}) copy-start(f32[64,4]{1,0:T(8,128)} %copy.91) | copy-start | bytes 3076
where the time goes:
time: 605 us; the launch traced here: 598 us
  matrix products  312 us (52%)
  waiting for transfers between devices  144 us (24%)
  local copies, waits for them, and re-layouts  98.8 us (16%)
  starting transfers between devices  29.5 us (5%)
  other arithmetic  12.7 us (2%)
    all_to_all x8, waiting for transfers between devices, exchange(): return lax.all_to_all(send_buf, GROUP_AXES, 1, 1, tiled=True)  144 us
    dot_general x2, matrix products, expert_backward(): jnp.einsum('lnf,ldf->lnd', d_up, w_up, preferred_element_type=jnp.float32)  50.5 us
    all_to_all x8, local copies, waits for them, and re-layouts, exchange(): return lax.all_to_all(send_buf, GROUP_AXES, 1, 1, tiled=True)  40.2 us
    dot_general x2, matrix products, expert_backward(): jnp.einsum('lnf,lnd->lfd', hidden, d_out, preferred_element_type=jnp.floa...  39.7 us
    dot_general x2, matrix products, expert_backward(): jnp.einsum('lnd,lnf->ldf', x_rows, d_gate, preferred_element_type=jnp.flo...  39.5 us
    dot_general x2, matrix products, expert_backward(): jnp.einsum('lnd,lnf->ldf', x_rows, d_up, preferred_element_type=jnp.float32)  39 us
    dot_general x2, matrix products, expert_backward(): jnp.einsum('lnf,ldf->lnd', d_gate, w_gate, preferred_element_type=jnp.flo...  31.7 us
    dot_general x2, matrix products, expert_backward(): jnp.einsum('lnd,lfd->lnf', d_out, w_down, preferred_element_type=jnp.floa...  31.2 us
  transfers between devices with their start and end apart: 8, of which 6 were waited for; matrix products, arithmetic and copies ran while one was open for 66% of the time, Pallas kernels for 0%

commit v1 on v0

v1 whole, which is shorter than its diff:
```python
import functools

import jax
import jax.numpy as jnp
from jax import lax
from jax.experimental import pallas as pl
from jax.experimental.pallas import tpu as pltpu
from jax.sharding import PartitionSpec as P

GROUP_AXES = ("row", "col", "core")
ALL_AXES = ("rep", "row", "col", "core")
MESH = pl.DeviceIdType.MESH
F32, BF16, I32 = jnp.float32, jnp.bfloat16, jnp.int32

N_DEV = 8
BLK = 128
TOK = N_DEV * BLK
TOP_K = 4
LOC = 16
DIM = 640
GATHER = 128
COMB = 256
SMALL, BIG = 64, 256
ROWS = 4864
SLAB = 640
RING = 4
VMEM_MAX = 67043328


def dot(a, b, dims=((1,), (0,))):
    return lax.dot_general(a, b, (dims, ((), ())), preferred_element_type=F32)


def gather_kernel(x_ref, gy_ref, meta_ref, xgy_ref, mall_ref, local_sem, send_sem, recv_sem):
    row, col, core = (lax.axis_index(a) for a in GROUP_AXES)
    sib = {"row": row, "col": col, "core": 1 - core}
    xn = {"row": row, "col": 1 - col, "core": core}
    yn = {"row": 1 - row, "col": col, "core": core}

    def index(r, c):
        return (r * 2 + c) * 2 + core

    blocks = {"own": index(row, col), "xn": index(row, 1 - col), "yn": index(1 - row, col), "diag": index(1 - row, 1 - col)}
    pair = {k: b + 1 - 2 * core for k, b in blocks.items()}
    pieces = ("x", "gy", "meta")

    def place(piece, blk):
        if piece == "meta":
            return mall_ref.at[blk]
        return xgy_ref.at[blk, :, pl.ds(0 if piece == "x" else DIM, DIM)]

    own_src = {"x": x_ref, "gy": gy_ref, "meta": meta_ref}

    barrier = pltpu.get_barrier_semaphore()
    for peer in (sib, xn, yn):
        pl.semaphore_signal(barrier, inc=1, device_id=peer, device_id_type=MESH)
    pl.semaphore_wait(barrier, 3)

    local = []
    for i, p in enumerate(pieces):
        local.append(pltpu.make_async_copy(own_src[p], place(p, blocks["own"]), local_sem.at[i]))
        local[-1].start()

    names = [("x", "own", p) for p in pieces] + [("y", "own", p) for p in pieces]
    names += [("x", "yn", "gy"), ("y", "xn", "x"), ("y", "xn", "meta")]
    names += [("s", b, p) for b in ("own", "xn", "yn", "diag") for p in pieces]
    number = {n: i for i, n in enumerate(names)}
    peer_of = {"x": xn, "y": yn, "s": sib}

    def copy(name):
        link, b, p = name
        i = number[name]
        src = own_src[p] if b == "own" else place(p, blocks[b])
        return pltpu.make_async_remote_copy(
            src_ref=src, dst_ref=place(p, blocks[b]), send_sem=send_sem.at[i], recv_sem=recv_sem.at[i],
            device_id=peer_of[link], device_id_type=MESH)

    copies = {n: copy(n) for n in names}
    for n in (("x", "own", "meta"), ("y", "own", "meta"), ("x", "own", "x"), ("y", "own", "gy"), ("x", "own", "gy"), ("y", "own", "x"),
              ("s", "own", "meta"), ("s", "own", "x"), ("s", "own", "gy")):
        copies[n].start()

    def arrived(link, b, p):
        copies[(link, b, p)].wait_recv()

    arrived("x", "own", "meta")
    copies[("y", "xn", "meta")].start()
    copies[("s", "xn", "meta")].start()
    arrived("y", "own", "meta")
    copies[("s", "yn", "meta")].start()
    arrived("x", "own", "x")
    copies[("y", "xn", "x")].start()
    copies[("s", "xn", "x")].start()
    arrived("y", "own", "gy")
    copies[("x", "yn", "gy")].start()
    copies[("s", "yn", "gy")].start()
    arrived("x", "own", "gy")
    copies[("s", "xn", "gy")].start()
    arrived("y", "own", "x")
    copies[("s", "yn", "x")].start()
    arrived("y", "xn", "meta")
    copies[("s", "diag", "meta")].start()
    arrived("y", "xn", "x")
    copies[("s", "diag", "x")].start()
    arrived("x", "yn", "gy")
    copies[("s", "diag", "gy")].start()
    for b in ("own", "xn", "yn", "diag"):
        for p in pieces:
            arrived("s", b, p)
    for n in names:
        copies[n].wait_send()
    for c in local:
        c.wait()


def all_gather_tokens(x_loc, gy_loc, meta):
    n_copies = 21
    vmem = pl.BlockSpec(memory_space=pltpu.VMEM)
    return pl.pallas_call(
        gather_kernel,
        out_shape=(jax.ShapeDtypeStruct((N_DEV, BLK, 2 * DIM), BF16), jax.ShapeDtypeStruct((N_DEV, 8, BLK), F32)),
        in_specs=[vmem] * 3,
        out_specs=(vmem, vmem),
        scratch_shapes=[pltpu.SemaphoreType.DMA((3,)), pltpu.SemaphoreType.DMA((n_copies,)), pltpu.SemaphoreType.DMA((n_copies,))],
        compiler_params=pltpu.CompilerParams(collective_id=0, has_side_effects=True),
        name="token_gather",
    )(x_loc, gy_loc, meta)


def expert_kernel(meta_ref, xgy_ref, wg_hbm, wu_hbm, wd_hbm, sy_ref, sdx_ref, rows_hbm, cnt_ref,
                  wgu, wd, xs, gys, gcol, os_, ps, dgcol, pos, pos_t, gate_row, off_s, stage_s, stage_b, w_sem, s_sem, b_sem):
    row, col, core = (lax.axis_index(a) for a in GROUP_AXES)
    first = ((row * 2 + col) * 2 + core) * LOC

    def weights(e):
        slot = lax.rem(e, RING)
        return (pltpu.make_async_copy(wg_hbm.at[e], wgu.at[slot, :, pl.ds(0, DIM)], w_sem.at[slot, 0]),
                pltpu.make_async_copy(wu_hbm.at[e], wgu.at[slot, :, pl.ds(DIM, DIM)], w_sem.at[slot, 1]),
                pltpu.make_async_copy(wd_hbm.at[e], wd.at[slot], w_sem.at[slot, 2]))

    for e in range(RING):
        for c in weights(jnp.int32(e)):
            c.start()

    local = [jnp.concatenate([meta_ref[n, j:j + 1, :] for n in range(N_DEV)], axis=1) - first.astype(F32) for j in range(TOP_K)]
    for j in range(TOP_K):
        gate_row[j:j + 1, :] = jnp.concatenate([meta_ref[n, TOP_K + j:TOP_K + j + 1, :] for n in range(N_DEV)], axis=1)
    eid = lax.broadcasted_iota(I32, (LOC, TOK), 0).astype(F32)
    member = jnp.zeros((LOC, TOK), F32)
    for j in range(TOP_K):
        member = member + jnp.where(local[j] == eid, 1.0, 0.0)
    upper = (lax.broadcasted_iota(I32, (BLK, BLK), 0) < lax.broadcasted_iota(I32, (BLK, BLK), 1))
    upper = jnp.where(upper, 1.0, 0.0).astype(BF16)
    parts = [member[:, b * BLK:(b + 1) * BLK] for b in range(N_DEV)]
    before = dot(jnp.concatenate(parts, axis=0).astype(BF16), upper)
    run = jnp.zeros((LOC, 1), F32)
    ranks = []
    for b in range(N_DEV):
        ranks.append(before[b * LOC:(b + 1) * LOC, :] + run)
        run = run + jnp.sum(parts[b], axis=1, keepdims=True)
    rank = jnp.concatenate(ranks, axis=1)
    erow = lax.broadcasted_iota(I32, (LOC, 1), 0)
    off_v = jnp.zeros((LOC, 1), F32)
    off = jnp.int32(0)
    for e in range(LOC):
        cnt = jnp.sum(jnp.where(erow == e, run, 0.0)).astype(I32)
        cnt_ref[e] = cnt
        off_s[e] = off
        off_v = jnp.where(erow == e, off.astype(F32), off_v)
        off = off + ((cnt + 15) // 16) * 16
    n_comb = (off + COMB - 1) // COMB
    place = rank + off_v
    for j in range(TOP_K):
        mine = jnp.full((1, TOK), -1.0, F32)
        for e in range(LOC):
            mine = jnp.where(local[j] == float(e), place[e:e + 1, :], mine)
        pos[j:j + 1, :] = mine
    for b in range(N_DEV):
        blk = jnp.concatenate([pos[:, b * BLK:(b + 1) * BLK], jnp.zeros((BLK - 8, BLK), F32)], axis=0)
        pos_t[b * BLK:(b + 1) * BLK, :] = blk.T

    sy_ref[...] = jnp.zeros_like(sy_ref)
    sdx_ref[...] = jnp.zeros_like(sdx_ref)

    def gather(i, carry):
        r0 = pl.multiple_of(i * GATHER, GATHER)
        rid = (r0 + lax.broadcasted_iota(I32, (GATHER, 1), 0)).astype(F32)
        picks, gsum = [], jnp.zeros((GATHER, 256), F32)
        for kb in range(TOK // 256):
            lanes = slice(kb * 256, (kb + 1) * 256)
            hit, gsel = None, gsum
            for j in range(TOP_K):
                m = pos[j:j + 1, lanes] == rid
                hit = m if hit is None else hit | m
                gsel = jnp.where(m, gate_row[j:j + 1, lanes], gsel)
            gsum = gsel
            picks.append(jnp.where(hit, 1.0, 0.0).astype(BF16))
        got = dot(jnp.concatenate(picks, axis=1), xgy_ref[...].reshape(TOK, 2 * DIM)).astype(BF16)
        here = pl.ds(r0, GATHER)
        xs[here, :] = got[:, :DIM]
        gys[here, :] = got[:, DIM:]
        gcol[here, :] = jnp.sum(gsum, axis=1, keepdims=True)
        os_[here, :] = jnp.zeros((GATHER, DIM), BF16)
        ps[here, :] = jnp.zeros((GATHER, DIM), BF16)
        dgcol[here, :] = jnp.zeros((GATHER, 1), F32)
        return carry

    lax.fori_loop(0, 2 * n_comb, gather, 0)

    def chunk(size, base, slot, stage):
        here = pl.ds(pl.multiple_of(base, 16), size)
        x = xs[here, :]
        gy = gys[here, :].astype(F32)
        q = (gcol[here, :] * gy).astype(BF16)
        uv = dot(x, wgu[slot])
        u = uv[:, :DIM].astype(BF16).astype(F32)
        v = uv[:, DIM:].astype(BF16).astype(F32)
        s = jax.nn.sigmoid(u)
        a = (u * s * v).astype(BF16)
        o = dot(a, wd[slot]).astype(BF16)
        r = dot(q, wd[slot], ((1,), (1,)))
        dv = (r * u * s).astype(BF16)
        du = (r * v * s * (1.0 + u * (1.0 - s))).astype(BF16)
        duv = jnp.concatenate([du, dv], axis=1)
        p = dot(duv, wgu[slot], ((1,), (1,))).astype(BF16)
        os_[here, :] = o
        ps[here, :] = p
        dgcol[here, :] = jnp.sum(gy * o.astype(F32), axis=1, keepdims=True)
        stage[:, 0:DIM] = x
        stage[:, DIM:2 * DIM] = a
        stage[:, 2 * DIM:3 * DIM] = q
        stage[:, 3 * DIM:5 * DIM] = duv

    def small_out(e, row0):
        return pltpu.make_async_copy(stage_s.at[lax.rem(e, 2)], rows_hbm.at[e, pl.ds(pl.multiple_of(row0, 64), SMALL)], s_sem.at[lax.rem(e, 2)])

    def expert(e, carry):
        slot = lax.rem(e, RING)
        cnt, base = cnt_ref[e], off_s[e]
        for c in weights(e):
            c.wait()
        n_big = (cnt + BIG - SMALL - 1) // BIG

        def big(b, c2):
            chunk(BIG, base + b * BIG, slot, stage_b)
            out = pltpu.make_async_copy(stage_b, rows_hbm.at[e, pl.ds(pl.multiple_of(b * BIG, BIG), BIG)], b_sem)
            out.start()
            out.wait()
            return c2

        lax.fori_loop(0, n_big, big, 0)

        @pl.when(e >= 2)
        def _():
            small_out(e, 0).wait()

        chunk(SMALL, base + n_big * BIG, slot, stage_s.at[lax.rem(e, 2)])
        small_out(e, n_big * BIG).start()

        @pl.when(e + RING < LOC)
        def _():
            for c in weights(e + RING):
                c.start()

        return carry

    lax.fori_loop(0, LOC, expert, 0)
    small_out(0, 0).wait()
    small_out(1, 0).wait()

    def combine(i, carry):
        r0 = pl.multiple_of(i * COMB, COMB)
        here = pl.ds(r0, COMB)
        go = gcol[here, :] * os_[here, :].astype(F32)
        hi = go.astype(BF16)
        rem = go - hi.astype(F32)
        mid = rem.astype(BF16)
        low = (rem - mid.astype(F32)).astype(BF16)
        triple = jnp.concatenate([hi, mid, low], axis=0)
        p = ps[here, :]
        dg = dgcol[here, :]
        rid_l = (r0 + lax.broadcasted_iota(I32, (1, COMB), 1)).astype(F32)
        rid_s = (r0 + lax.broadcasted_iota(I32, (COMB, 1), 0)).astype(F32)
        for r in range(2):
            for c in range(2):
                for k in range(2):
                    n = (r * 2 + c) * 2 + k
                    toks = slice(n * BLK, (n + 1) * BLK)
                    hit = None
                    for j in range(TOP_K):
                        m = pos_t[toks, j:j + 1] == rid_l
                        hit = m if hit is None else hit | m
                    pick = jnp.where(hit, 1.0, 0.0).astype(BF16)
                    far = lax.rem(core + k, 2)
                    rel = lax.rem(row + r, 2) * 2 + lax.rem(col + c, 2)
                    sy_ref[far, rel, 0:BLK, :] += dot(jnp.concatenate([pick] * 3, axis=1), triple)
                    sdx_ref[far, rel, :, :] += dot(pick, p)
                    for j in range(TOP_K):
                        m = pos[j:j + 1, toks] == rid_s
                        sy_ref[far, rel, BLK + j:BLK + j + 1, 0:BLK] += jnp.sum(jnp.where(m, dg, 0.0), axis=0, keepdims=True)
        return carry

    lax.fori_loop(0, n_comb, combine, 0)


def run_experts(meta_all, xgy, w_gate, w_up, w_down):
    vmem = pl.BlockSpec(memory_space=pltpu.VMEM)
    hbm = pl.BlockSpec(memory_space=pl.ANY)
    return pl.pallas_call(
        expert_kernel,
        out_shape=(jax.ShapeDtypeStruct((2, 4, BLK + 8, DIM), F32), jax.ShapeDtypeStruct((2, 4, BLK, DIM), F32),
                   jax.ShapeDtypeStruct((LOC, SLAB, 5 * DIM), BF16), jax.ShapeDtypeStruct((LOC,), I32)),
        in_specs=[vmem, vmem, hbm, hbm, hbm],
        out_specs=(vmem, vmem, hbm, pl.BlockSpec(memory_space=pltpu.SMEM)),
        scratch_shapes=[
            pltpu.VMEM((RING, DIM, 2 * DIM), BF16), pltpu.VMEM((RING, DIM, DIM), BF16),
            pltpu.VMEM((ROWS, DIM), BF16), pltpu.VMEM((ROWS, DIM), BF16), pltpu.VMEM((ROWS, 1), F32),
            pltpu.VMEM((ROWS, DIM), BF16), pltpu.VMEM((ROWS, DIM), BF16), pltpu.VMEM((ROWS, 1), F32),
            pltpu.VMEM((8, TOK), F32), pltpu.VMEM((TOK, BLK), F32), pltpu.VMEM((8, TOK), F32),
            pltpu.SMEM((LOC,), I32),
            pltpu.VMEM((2, SMALL, 5 * DIM), BF16), pltpu.VMEM((BIG, 5 * DIM), BF16),
            pltpu.SemaphoreType.DMA((RING, 3)), pltpu.SemaphoreType.DMA((2,)), pltpu.SemaphoreType.DMA,
        ],
        compiler_params=pltpu.CompilerParams(vmem_limit_bytes=VMEM_MAX),
        cost_estimate=pl.CostEstimate(flops=6_000_000_000, bytes_accessed=60_000_000, transcendentals=0),
        name="expert_rows",
    )(meta_all, xgy, w_gate, w_up, w_down)


def wgrad_kernel(lo, hi, n_alias, cnt_ref, rows_hbm, *refs):
    gg_hbm, gu_hbm, gd_hbm = refs[n_alias:n_alias + 3]
    small, big, out_gu, out_d, r_sem, b_sem, o_sem = refs[n_alias + 3:]

    def rows_in(i):
        return pltpu.make_async_copy(rows_hbm.at[lo + i, pl.ds(0, SMALL)], small.at[lax.rem(i, 2)], r_sem.at[lax.rem(i, 2)])

    def results(i):
        slot, e = lax.rem(i, 2), lo + i
        return (pltpu.make_async_copy(out_gu.at[slot, :, pl.ds(0, DIM)], gg_hbm.at[e], o_sem.at[slot, 0]),
                pltpu.make_async_copy(out_gu.at[slot, :, pl.ds(DIM, DIM)], gu_hbm.at[e], o_sem.at[slot, 1]),
                pltpu.make_async_copy(out_d.at[slot], gd_hbm.at[e], o_sem.at[slot, 2]))

    def products(ref, size, left):
        keep = lax.broadcasted_iota(I32, (size, 1), 0) < left
        part = lambda a, b: jnp.where(keep, ref[:, a * DIM:b * DIM], 0.0).astype(BF16)
        x, a, q, duv = part(0, 1), part(1, 2), part(2, 3), part(3, 5)
        return dot(x, duv, ((0,), (0,))), dot(a, q, ((0,), (0,)))

    rows_in(0).start()

    def expert(i, carry):
        slot = lax.rem(i, 2)
        cnt = cnt_ref[lo + i]
        rows_in(i).wait()

        @pl.when(i + 1 < hi - lo)
        def _():
            rows_in(i + 1).start()

        @pl.when(i >= 2)
        def _():
            for c in results(i - 2):
                c.wait()

        @pl.when(cnt <= SMALL)
        def _():
            g1, g2 = products(small.at[slot], SMALL, cnt)
            out_gu[slot] = g1
            out_d[slot] = g2

        @pl.when(cnt > SMALL)
        def _():
            def piece(b, c2):
                cp = pltpu.make_async_copy(rows_hbm.at[lo + i, pl.ds(pl.multiple_of(b * BIG, BIG), BIG)], big, b_sem)
                cp.start()
                cp.wait()
                g1, g2 = products(big, BIG, cnt - b * BIG)

                @pl.when(b == 0)
                def _():
                    out_gu[slot] = g1
                    out_d[slot] = g2

                @pl.when(b > 0)
                def _():
                    out_gu[slot] += g1
                    out_d[slot] += g2

                return c2

            lax.fori_loop(0, (cnt + BIG - 1) // BIG, piece, 0)

        for c in results(i):
            c.start()
        return carry

    lax.fori_loop(0, hi - lo, expert, 0)
    for i in (hi - lo - 2, hi - lo - 1):
        for c in results(jnp.int32(i)):
            c.wait()


def weight_grads(lo, hi, cnt, rows, earlier=()):
    hbm = pl.BlockSpec(memory_space=pl.ANY)
    out = jax.ShapeDtypeStruct((LOC, DIM, DIM), F32)
    return pl.pallas_call(
        functools.partial(wgrad_kernel, lo, hi, len(earlier)),
        out_shape=(out, out, out),
        in_specs=[pl.BlockSpec(memory_space=pltpu.SMEM), hbm] + [hbm] * len(earlier),
        out_specs=(hbm, hbm, hbm),
        input_output_aliases={2 + i: i for i in range(len(earlier))},
        scratch_shapes=[
            pltpu.VMEM((2, SMALL, 5 * DIM), BF16), pltpu.VMEM((BIG, 5 * DIM), BF16),
            pltpu.VMEM((2, DIM, 2 * DIM), F32), pltpu.VMEM((2, DIM, DIM), F32),
            pltpu.SemaphoreType.DMA((2,)), pltpu.SemaphoreType.DMA, pltpu.SemaphoreType.DMA((2, 3)),
        ],
        compiler_params=pltpu.CompilerParams(vmem_limit_bytes=30 * 1024 * 1024),
        cost_estimate=pl.CostEstimate(flops=(hi - lo) * 400_000_000, bytes_accessed=(hi - lo) * 5_000_000, transcendentals=0),
        name="weight_grads",
    )(cnt, rows, *earlier)


def solution(mesh):
    tok_spec = P(None, ALL_AXES, None)
    w_spec = P(ALL_AXES, None, None)

    def swap(value, axis):
        return lax.ppermute(value, axis, [(0, 1), (1, 0)])

    def moe_layer(x, route_idx, gates, w_gate, w_up, w_down, grad_y):
        tok_dev = x.shape[1]
        flat = lambda a: a.reshape(2 * tok_dev, -1)
        meta = jnp.concatenate([flat(route_idx).astype(F32).T, flat(gates).T], axis=0)
        xgy, meta_all = all_gather_tokens(flat(x), flat(grad_y), meta)
        sum_y, sum_dx, rows, cnt = run_experts(meta_all, xgy, w_gate, w_up, w_down)
        chip_y = sum_y[0] + swap(sum_y[1], "core")
        chip_dx = sum_dx[0] + swap(sum_dx[1], "core")
        y_in = swap(chip_y[1::2], "col")
        dx_in = swap(chip_dx[2:], "row")
        early = weight_grads(0, 10, cnt, rows)
        y_far = swap(chip_y[2] + y_in[1], "row")
        dx_far = swap(chip_dx[1] + dx_in[1], "col")
        g_gate, g_up, g_down = weight_grads(10, LOC, cnt, rows, early)
        y_sum = chip_y[0] + y_in[0] + y_far
        dx_sum = chip_dx[0] + dx_in[0] + dx_far
        y = y_sum[:BLK].astype(BF16).reshape(x.shape)
        dx = dx_sum.astype(BF16).reshape(x.shape)
        dg = y_sum[BLK:BLK + TOP_K, :BLK].T.reshape(gates.shape)
        return y, dx, dg, g_gate, g_up, g_down

    return jax.shard_map(moe_layer, mesh=mesh, in_specs=(tok_spec, tok_spec, tok_spec, w_spec, w_spec, w_spec, tok_spec), out_specs=(tok_spec, tok_spec, tok_spec, w_spec, w_spec, w_spec), check_vma=False)
```

time: 605 us -> 114 us (0.19); the launches traced: 598 us -> 114 us
  matrix products: 312 us -> 0 us
  waiting for transfers between devices: 144 us -> 0.97 us
  local copies, waits for them, and re-layouts: 98.8 us -> 5.33 us
  Pallas kernels: 0 us -> 87.9 us
  starting transfers between devices: 29.5 us -> 16.5 us
  other arithmetic: 12.7 us -> 2.49 us
    dot_general x24 -> x0, matrix products: 312 us -> none  [the longest x2 50.5 us: expert_backward(): jnp.einsum('lnf,ldf->lnd', d_up, w_up, preferred_element_type=jnp.float32)]
    all_to_all x8 -> x0, waiting for transfers between devices: 144 us -> none  [exchange(): return lax.all_to_all(send_buf, GROUP_AXES, 1, 1, tiled=True)]
    pallas_call x0 -> x4, Pallas kernels: none -> 87.9 us  [the longest x1 36.9 us: run_experts(): pl.pallas_call(expert_kernel, out_shape=(jax.ShapeDtypeStruct((2, 4, BLK...]
    all_to_all x8 -> x0, local copies, waits for them, and re-layouts: 40.2 us -> none  [exchange(): return lax.all_to_all(send_buf, GROUP_AXES, 1, 1, tiled=True)]
    all_to_all x8 -> x0, starting transfers between devices: 29.5 us -> none  [exchange(): return lax.all_to_all(send_buf, GROUP_AXES, 1, 1, tiled=True)]
    reshape x4 -> x2, local copies, waits for them, and re-layouts: 19.3 us -> 0.17 us  [the longest x1 0.08 us: moe_layer(): flat = lambda a: a.reshape(2 * tok_dev, -1)]
    gather x8 -> x0, local copies, waits for them, and re-layouts: 18.2 us -> none  [the longest x4 9.13 us: moe_layer(): out_slots = jnp.take(out_back, slot_addr, axis=0)]
    ppermute x0 -> x6, starting transfers between devices: none -> 16.5 us  [swap(): return lax.ppermute(value, axis, [(0, 1), (1, 0)])]
  transfers between devices with their start and end apart: 8 -> 6, of which waited for: 6 -> 1; matrix products, arithmetic and copies ran while one was open for 66% -> 2% of each run, Pallas kernels for 0% -> 27%
where the time goes in v1:
time: 114 us
  Pallas kernels  87.9 us (77%)
  starting transfers between devices  16.5 us (14%)
  local copies, waits for them, and re-layouts  5.33 us (5%)
  other arithmetic  2.49 us (2%)
    pallas_call x1, Pallas kernels, run_experts(): pl.pallas_call(expert_kernel, out_shape=(jax.ShapeDtypeStruct((2, 4, BLK...  36.9 us
    pallas_call x2, Pallas kernels, weight_grads(): pl.pallas_call(functools.partial(wgrad_kernel, lo, hi, len(earlier)), out...  30.8 us
    pallas_call x1, Pallas kernels, all_gather_tokens(): pl.pallas_call(gather_kernel, out_shape=(jax.ShapeDtypeStruct((N_DEV, BLK...  20.2 us
    ppermute x6, starting transfers between devices, swap(): return lax.ppermute(value, axis, [(0, 1), (1, 0)])  16.5 us
  transfers between devices with their start and end apart: 6, of which 1 were waited for; matrix products, arithmetic and copies ran while one was open for 2% of the time, Pallas kernels for 27%

profile of v1, /device:TPU:0, one launch (start us, length us, event | category | flops | bytes accessed | tf_op | source)
XLA Modules:
  0.0 113.9 jit_solution(1503612497325409209)
XLA Ops:
  0.6 0.7 convert_element_type.10
  1.3 0.1 convert_element_type.11
  1.4 0.7 copy.17
  2.1 0.1 reshape.38
  2.2 0.6 pad_maximum_fusion.meta_ref
  2.8 20.2 %token_gather.1 = (bf16[8,128,1280]{2,1,0:T(8,128)(2,1)}, f32[8,8,128]{2,1,0:T(8,128)}) custom-call(bf16[128,640]{1,0:T(8,128)(2,1)} %bitcast.38, bf16[128,640]{1,0:T(8,128)(2,1)} %bitcast.39, f32[8,128]{1,0:T(8,128)} %pad_maximum_fusion.meta_ref), custom_call_target="tpu_custom_call" | custom-call | tf_op jit(solution)/shard_map/token_gather/pallas_call | solution.py:119
  23.0 36.9 %expert_rows.1 = (f32[2,4,136,640]{3,2,1,0:T(8,128)}, f32[2,4,128,640]{3,2,1,0:T(8,128)}, bf16[16,640,3200]{2,1,0:T(8,128)(2,1)}, s32[16]{0:T(128)}) custom-call(f32[8,8,128]{2,1,0:T(8,128)} %get-tuple-element.18.meta_ref, bf16[8,128,1280]{2,1,0:T(8,128)(2,1)} %get-tuple-element.19.xgy_ref, bf16[16,640,640]{2,1,0:T(8,128)(2,1)} %wg_hbm.1, ...), custom_call_target="tpu_custom_call" | custom-call | flops 6000000000 | bytes 60000000 | tf_op jit(solution)/shard_map/expert_rows/pallas_call | solution.py:309
  59.9 1.4 %slice_bitcast_fusion.1 = f32[4,128,640]{2,1,0:T(8,128)S(1)} fusion(f32[2,4,128,640]{3,2,1,0:T(8,128)} %get-tuple-element.21), kind=kLoop, calls=%fused_computation.3 | loop fusion | bytes 2621440 | tf_op jit(solution)/shard_map/squeeze | solution.py:437
  61.3 0.4 collective-permute-start.3
  61.7 0.0 copy-start.2
  61.7 1.6 %slice_bitcast_fusion = f32[4,136,640]{2,1,0:T(8,128)S(1)} fusion(f32[2,4,136,640]{3,2,1,0:T(8,128)} %get-tuple-element.20), kind=kLoop, calls=%fused_computation.1 | loop fusion | bytes 2785280 | tf_op jit(solution)/shard_map/squeeze | solution.py:436
  63.3 0.1 collective-permute-start
  63.4 1.0 collective-permute-done.3
  64.4 0.0 copy-done.2
  64.4 0.0 copy-start.1
  64.4 0.1 bitcast_add_fusion.1
  64.6 8.4 %collective-permute-start.4 = (f32[2,128,640]{2,1,0:T(8,128)S(1)}, f32[2,128,640]{2,1,0:T(8,128)S(1)}, u32[]{:S(2)}, u32[]{:S(2)}) collective-permute-start(f32[2,128,640]{2,1,0:T(8,128)S(1)} %slice.71), channel_id=1, source_target_pairs={{0,4},{4,0},{1,5},{5,1},{2,6},{6,2},{3,7},{7,3}} | collective-permute-start | bytes 1966088 | tf_op jit(solution)/shard_map/ppermute | solution.py:428
  73.0 0.0 collective-permute-done
  73.0 0.0 copy-done.1
  73.0 0.1 bitcast_add_fusion
  73.1 0.0 copy-start
  73.2 2.2 %collective-permute-start.1 = (f32[2,136,640]{2,1,0:T(8,128)S(1)}, f32[2,136,640]{2,1,0:T(8,128)S(1)}, u32[]{:S(2)}, u32[]{:S(2)}) collective-permute-start(f32[2,136,640]{2,1,0:T(8,128)S(1)} %slice.52), channel_id=1, source_target_pairs={{0,2},{2,0},{1,3},{3,1},{4,6},{6,4},{5,7},{7,5}} | collective-permute-start | bytes 2088968 | tf_op jit(solution)/shard_map/ppermute | solution.py:428
  75.4 0.0 copy-done
  75.4 18.6 %weight_grads.2 = (f32[16,640,640]{2,1,0:T(8,128)}, f32[16,640,640]{2,1,0:T(8,128)}, f32[16,640,640]{2,1,0:T(8,128)}) custom-call(s32[16]{0:T(128)S(1)} %copy-done, bf16[16,640,3200]{2,1,0:T(8,128)(2,1)} %get-tuple-element.23.rows_hbm), custom_call_target="tpu_custom_call" | custom-call | flops 4000000000 | bytes 50000000 | tf_op jit(solution)/shard_map/weight_grads/pallas_call | solution.py:406
  94.1 0.0 collective-permute-done.4
  94.1 5.3 %collective-permute-start.5 = (f32[128,640]{1,0:T(8,128)S(1)}, f32[128,640]{1,0:T(8,128)S(1)}, u32[]{:S(2)}, u32[]{:S(2)}) collective-permute-start(f32[128,640]{1,0:T(8,128)S(1)} %fusion.3), channel_id=1, source_target_pairs={{0,2},{2,0},{1,3},{3,1},{4,6},{6,4},{5,7},{7,5}} | collective-permute-start | bytes 983048 | tf_op jit(solution)/shard_map/ppermute | solution.py:428
  99.4 0.0 collective-permute-done.1
  99.5 0.1 fusion
  99.5 0.0 collective-permute-start.2
  99.5 12.2 %weight_grads.3 = (f32[16,640,640]{2,1,0:T(8,128)}, f32[16,640,640]{2,1,0:T(8,128)}, f32[16,640,640]{2,1,0:T(8,128)}) custom-call(s32[16]{0:T(128)S(1)} %copy-done, bf16[16,640,3200]{2,1,0:T(8,128)(2,1)} %get-tuple-element.23.rows_hbm, f32[16,640,640]{2,1,0:T(8,128)} %get-tuple-element.24.refs_0_, ...), custom_call_target="tpu_custom_call", output_to_operand_aliasing={{0}: (2, {}), {1}: (3, {}), {2}: (4, {})} | custom-call | flops 2400000000 | bytes 30000000 | tf_op jit(solution)/shard_map/weight_grads/pallas_call | solution.py:406
  111.7 0.0 collective-permute-done.5
  111.8 0.7 fusion.6
  112.5 0.0 collective-permute-done.2
  112.5 0.1 fusion.2
  112.6 0.7 slice.104
  113.3 0.1 reshape.41
  113.3 0.6 copy.18
  (5 shorter events, 0.1 us)
Async XLA Ops:
  61.3 3.1 %collective-permute-start.3 = (f32[4,128,640]{2,1,0:T(8,128)S(1)}, f32[4,128,640]{2,1,0:T(8,128)S(1)}, u32[]{:S(2)}, u32[]{:S(2)}) collective-permute-start(f32[4,128,640]{2,1,0:T(8,128)S(1)} %slice_bitcast_fusion.1), channel_id=1, source_target_pairs={{0,1},{1,0},{2,3},{3,2},{4,5},{5,4},{6,7},{7,6}} | collective-permute-start | bytes 3932168 | tf_op jit(solution)/shard_map/ppermute | solution.py:428
  61.7 2.7 %copy-start.2 = (f32[2,4,128,640]{3,2,1,0:T(8,128)S(1)}, f32[2,4,128,640]{3,2,1,0:T(8,128)}, u32[]{:S(2)}) copy-start(f32[2,4,128,640]{3,2,1,0:T(8,128)} %get-tuple-element.21) | copy-start | bytes 7864324
  63.3 9.7 %collective-permute-start = (f32[4,136,640]{2,1,0:T(8,128)S(1)}, f32[4,136,640]{2,1,0:T(8,128)S(1)}, u32[]{:S(2)}, u32[]{:S(2)}) collective-permute-start(f32[4,136,640]{2,1,0:T(8,128)S(1)} %slice_bitcast_fusion), channel_id=1, source_target_pairs={{0,1},{1,0},{2,3},{3,2},{4,5},{5,4},{6,7},{7,6}} | collective-permute-start | bytes 4177928 | tf_op jit(solution)/shard_map/ppermute | solution.py:428
  64.4 8.6 %copy-start.1 = (f32[2,4,136,640]{3,2,1,0:T(8,128)S(1)}, f32[2,4,136,640]{3,2,1,0:T(8,128)}, u32[]{:S(2)}) copy-start(f32[2,4,136,640]{3,2,1,0:T(8,128)} %get-tuple-element.20) | copy-start | bytes 8355844
  64.6 29.5 %collective-permute-start.4 = (f32[2,128,640]{2,1,0:T(8,128)S(1)}, f32[2,128,640]{2,1,0:T(8,128)S(1)}, u32[]{:S(2)}, u32[]{:S(2)}) collective-permute-start(f32[2,128,640]{2,1,0:T(8,128)S(1)} %slice.71), channel_id=1, source_target_pairs={{0,4},{4,0},{1,5},{5,1},{2,6},{6,2},{3,7},{7,3}} | collective-permute-start | bytes 1966088 | tf_op jit(solution)/shard_map/ppermute | solution.py:428
  73.1 2.3 %copy-start = (s32[16]{0:T(128)S(1)}, s32[16]{0:T(128)}, u32[]{:S(2)}) copy-start(s32[16]{0:T(128)} %get-tuple-element.22.cnt_ref) | copy-start | bytes 196
  73.2 26.2 %collective-permute-start.1 = (f32[2,136,640]{2,1,0:T(8,128)S(1)}, f32[2,136,640]{2,1,0:T(8,128)S(1)}, u32[]{:S(2)}, u32[]{:S(2)}) collective-permute-start(f32[2,136,640]{2,1,0:T(8,128)S(1)} %slice.52), channel_id=1, source_target_pairs={{0,2},{2,0},{1,3},{3,1},{4,6},{6,4},{5,7},{7,5}} | collective-permute-start | bytes 2088968 | tf_op jit(solution)/shard_map/ppermute | solution.py:428
  94.1 17.6 %collective-permute-start.5 = (f32[128,640]{1,0:T(8,128)S(1)}, f32[128,640]{1,0:T(8,128)S(1)}, u32[]{:S(2)}, u32[]{:S(2)}) collective-permute-start(f32[128,640]{1,0:T(8,128)S(1)} %fusion.3), channel_id=1, source_target_pairs={{0,2},{2,0},{1,3},{3,1},{4,6},{6,4},{5,7},{7,5}} | collective-permute-start | bytes 983048 | tf_op jit(solution)/shard_map/ppermute | solution.py:428
  99.5 13.0 %collective-permute-start.2 = (f32[136,640]{1,0:T(8,128)S(1)}, f32[136,640]{1,0:T(8,128)S(1)}, u32[]{:S(2)}, u32[]{:S(2)}) collective-permute-start(f32[136,640]{1,0:T(8,128)S(1)} %fusion), channel_id=1, source_target_pairs={{0,4},{4,0},{1,5},{5,1},{2,6},{6,2},{3,7},{7,3}} | collective-permute-start | bytes 1044488 | tf_op jit(solution)/shard_map/ppermute | solution.py:428

commit v2 on v1

v2 whole, which is shorter than its diff:
```python
import functools

import jax
import jax.numpy as jnp
from jax import lax
from jax.experimental import pallas as pl
from jax.experimental.pallas import tpu as pltpu
from jax.sharding import PartitionSpec as P

GROUP_AXES = ("row", "col", "core")
ALL_AXES = ("rep", "row", "col", "core")
MESH = pl.DeviceIdType.MESH
F32, BF16, I32 = jnp.float32, jnp.bfloat16, jnp.int32

N_DEV = 8
BLK = 128
TOK = N_DEV * BLK
TOP_K = 4
LOC = 16
DIM = 640
GATHER = 128
COMB = 256
SMALL, BIG = 32, 256
ROWS = 4864
SLAB = 640
RING = 4
PIECE = 288
VMEM_MAX = 67043328


def dot(a, b, dims=((1,), (0,))):
    return lax.dot_general(a, b, (dims, ((), ())), preferred_element_type=F32)


def gather_kernel(x_hbm, gy_hbm, route_ref, gate_ref, xg_hbm, mall_ref, land, own_meta, in_sem, out_sem, meta_sem, send_sem, recv_sem):
    row, col, core = (lax.axis_index(a) for a in GROUP_AXES)
    sib = {"row": row, "col": col, "core": 1 - core}
    xn = {"row": row, "col": 1 - col, "core": core}
    yn = {"row": 1 - row, "col": col, "core": core}

    def index(r, c):
        return (r * 2 + c) * 2 + core

    blocks = {"own": index(row, col), "xn": index(row, 1 - col), "yn": index(1 - row, col), "diag": index(1 - row, 1 - col)}
    pair = {k: b + 1 - 2 * core for k, b in blocks.items()}
    pieces = ("x", "gy", "meta")

    def place(piece, blk):
        if piece == "meta":
            return mall_ref.at[blk]
        return land.at[0 if piece == "x" else 1, blk]

    loads = [pltpu.make_async_copy(x_hbm, place("x", blocks["own"]), in_sem.at[0]),
             pltpu.make_async_copy(gy_hbm, place("gy", blocks["own"]), in_sem.at[1])]
    for c in loads:
        c.start()
    own_meta[0:TOP_K, :] = jnp.concatenate([route_ref[0], route_ref[1]], axis=1).astype(F32)
    own_meta[TOP_K:2 * TOP_K, :] = jnp.concatenate([gate_ref[0], gate_ref[1]], axis=1)

    barrier = pltpu.get_barrier_semaphore()
    for peer in (sib, xn, yn):
        pl.semaphore_signal(barrier, inc=1, device_id=peer, device_id_type=MESH)
    pl.semaphore_wait(barrier, 3)

    meta_copy = pltpu.make_async_copy(own_meta, place("meta", blocks["own"]), meta_sem)
    meta_copy.start()

    names = [("x", "own", p) for p in pieces] + [("y", "own", p) for p in pieces]
    names += [("x", "yn", "gy"), ("y", "xn", "x"), ("y", "xn", "meta")]
    names += [("s", b, p) for b in ("own", "xn", "yn", "diag") for p in pieces]
    number = {n: i for i, n in enumerate(names)}
    peer_of = {"x": xn, "y": yn, "s": sib}

    def copy(name):
        link, b, p = name
        i = number[name]
        src = own_meta if b == "own" and p == "meta" else place(p, blocks[b])
        return pltpu.make_async_remote_copy(
            src_ref=src, dst_ref=place(p, blocks[b]), send_sem=send_sem.at[i], recv_sem=recv_sem.at[i],
            device_id=peer_of[link], device_id_type=MESH)

    copies = {n: copy(n) for n in names}
    stores = []

    def store(p, blk):
        half = 0 if p == "x" else 1
        stores.append(pltpu.make_async_copy(land.at[half, blk], xg_hbm.at[half, blk], out_sem.at[len(stores)]))
        stores[-1].start()

    copies[("x", "own", "meta")].start()
    copies[("y", "own", "meta")].start()
    copies[("s", "own", "meta")].start()
    loads[0].wait()
    copies[("x", "own", "x")].start()
    loads[1].wait()
    for n in (("y", "own", "gy"), ("x", "own", "gy"), ("y", "own", "x"), ("s", "own", "x"), ("s", "own", "gy")):
        copies[n].start()
    store("x", blocks["own"])
    store("gy", blocks["own"])

    def arrived(link, b, p, onward, blk):
        copies[(link, b, p)].wait_recv()
        for n in onward:
            copies[n].start()
        if p != "meta":
            store(p, blk)

    arrived("x", "own", "meta", [("y", "xn", "meta"), ("s", "xn", "meta")], None)
    arrived("y", "own", "meta", [("s", "yn", "meta")], None)
    arrived("x", "own", "x", [("y", "xn", "x"), ("s", "xn", "x")], blocks["xn"])
    arrived("y", "own", "gy", [("x", "yn", "gy"), ("s", "yn", "gy")], blocks["yn"])
    arrived("s", "own", "x", [], pair["own"])
    arrived("s", "own", "gy", [], pair["own"])
    arrived("s", "xn", "x", [], pair["xn"])
    arrived("s", "yn", "gy", [], pair["yn"])
    arrived("x", "own", "gy", [("s", "xn", "gy")], blocks["xn"])
    arrived("y", "own", "x", [("s", "yn", "x")], blocks["yn"])
    arrived("y", "xn", "meta", [("s", "diag", "meta")], None)
    arrived("s", "xn", "gy", [], pair["xn"])
    arrived("s", "yn", "x", [], pair["yn"])
    arrived("y", "xn", "x", [("s", "diag", "x")], blocks["diag"])
    arrived("x", "yn", "gy", [("s", "diag", "gy")], blocks["diag"])
    for b in ("own", "xn", "yn", "diag"):
        arrived("s", b, "meta", [], None)
    arrived("s", "diag", "x", [], pair["diag"])
    arrived("s", "diag", "gy", [], pair["diag"])
    for n in names:
        copies[n].wait_send()
    meta_copy.wait()
    for c in stores:
        c.wait()


def all_gather_tokens(x_loc, gy_loc, route, gates):
    n_copies = 21
    vmem = pl.BlockSpec(memory_space=pltpu.VMEM)
    hbm = pl.BlockSpec(memory_space=pl.ANY)
    return pl.pallas_call(
        gather_kernel,
        out_shape=(jax.ShapeDtypeStruct((2, N_DEV, BLK, DIM), BF16), jax.ShapeDtypeStruct((N_DEV, 8, BLK), F32)),
        in_specs=[hbm, hbm, vmem, vmem],
        out_specs=(hbm, vmem),
        scratch_shapes=[pltpu.VMEM((2, N_DEV, BLK, DIM), BF16), pltpu.VMEM((8, BLK), F32), pltpu.SemaphoreType.DMA((2,)),
                        pltpu.SemaphoreType.DMA((16,)), pltpu.SemaphoreType.DMA,
                        pltpu.SemaphoreType.DMA((n_copies,)), pltpu.SemaphoreType.DMA((n_copies,))],
        compiler_params=pltpu.CompilerParams(collective_id=0, has_side_effects=True),
        name="token_gather",
    )(x_loc, gy_loc, route, gates)


def three_parts(value):
    hi = value.astype(BF16).astype(F32)
    mid = (value - hi).astype(BF16).astype(F32)
    return hi, mid, value - hi - mid


def expert_kernel(meta_ref, xg_hbm, wg_hbm, wu_hbm, wd_hbm, keep_y, send_y, keep_dx, send_dx, rows_hbm, cnt_ref,
                  xgy, mt, wgu, wd, xs, gys, mrow, os_, ps, gcol, pos, pos_t, tri, sy, sdx, dacc, off_s, stage_s, stage_b,
                  x_sem, w_sem, s_sem, b_sem, out_sem):
    row, col, core = (lax.axis_index(a) for a in GROUP_AXES)
    first = ((row * 2 + col) * 2 + core) * LOC

    def weights(e):
        slot = lax.rem(e, RING)
        return (pltpu.make_async_copy(wg_hbm.at[e], wgu.at[slot, :, pl.ds(0, DIM)], w_sem.at[slot, 0]),
                pltpu.make_async_copy(wu_hbm.at[e], wgu.at[slot, :, pl.ds(DIM, DIM)], w_sem.at[slot, 1]),
                pltpu.make_async_copy(wd_hbm.at[e], wd.at[slot], w_sem.at[slot, 2]))

    tokens_in = [pltpu.make_async_copy(xg_hbm.at[h], xgy.at[h], x_sem.at[h]) for h in range(2)]
    for c in tokens_in:
        c.start()
    for e in range(RING):
        for c in weights(jnp.int32(e)):
            c.start()

    local = [jnp.concatenate([meta_ref[n, j:j + 1, :] for n in range(N_DEV)], axis=1) - first.astype(F32) for j in range(TOP_K)]
    gate = jnp.concatenate([meta_ref[n, TOP_K:2 * TOP_K, :] for n in range(N_DEV)], axis=1)
    eid = lax.broadcasted_iota(I32, (LOC, TOK), 0).astype(F32)
    member = jnp.zeros((LOC, TOK), F32)
    for j in range(TOP_K):
        member = member + jnp.where(local[j] == eid, 1.0, 0.0)
    upper = (lax.broadcasted_iota(I32, (BLK, BLK), 0) < lax.broadcasted_iota(I32, (BLK, BLK), 1))
    upper = jnp.where(upper, 1.0, 0.0).astype(BF16)
    parts = [member[:, b * BLK:(b + 1) * BLK] for b in range(N_DEV)]
    before = dot(jnp.concatenate(parts, axis=0).astype(BF16), upper)
    run = jnp.zeros((LOC, 1), F32)
    ranks = []
    for b in range(N_DEV):
        ranks.append(before[b * LOC:(b + 1) * LOC, :] + run)
        run = run + jnp.sum(parts[b], axis=1, keepdims=True)
    rank = jnp.concatenate(ranks, axis=1)
    erow = lax.broadcasted_iota(I32, (LOC, 1), 0)
    off_v = jnp.zeros((LOC, 1), F32)
    off = jnp.int32(0)
    for e in range(LOC):
        cnt = jnp.sum(jnp.where(erow == e, run, 0.0)).astype(I32)
        cnt_ref[e] = cnt
        off_s[e] = off
        off_v = jnp.where(erow == e, off.astype(F32), off_v)
        off = off + ((cnt + 15) // 16) * 16
    n_comb = jnp.maximum((off + COMB - 1) // COMB, 1)
    place = rank + off_v
    for j in range(TOP_K):
        mine = jnp.full((1, TOK), -1.0, F32)
        for e in range(LOC):
            mine = jnp.where(local[j] == float(e), place[e:e + 1, :], mine)
        pos[j:j + 1, :] = mine
    ids = jnp.concatenate(local, axis=0)
    gap = jnp.zeros((TOP_K, TOK), F32)
    slots = jnp.concatenate([*three_parts(gate), gap, ids, ids, ids, gap, pos[0:TOP_K, :], jnp.zeros((BLK - 36, TOK), F32)], axis=0)
    for b in range(N_DEV):
        turned = slots[:, b * BLK:(b + 1) * BLK].T
        pos_t[b * BLK:(b + 1) * BLK, :] = turned
        mt[b * BLK:(b + 1) * BLK, :] = turned.astype(BF16)

    sy[...] = jnp.zeros_like(sy)
    sdx[...] = jnp.zeros_like(sdx)
    dacc[...] = jnp.zeros_like(dacc)
    for c in tokens_in:
        c.wait()

    def gather(i, carry):
        r0 = pl.multiple_of(i * GATHER, GATHER)
        rid = (r0 + lax.broadcasted_iota(I32, (GATHER, 1), 0)).astype(F32)
        here = pl.ds(r0, GATHER)
        picks = []
        for kb in range(TOK // 256):
            lanes = slice(kb * 256, (kb + 1) * 256)
            hit = None
            for j in range(TOP_K):
                m = pos[j:j + 1, lanes] == rid
                hit = m if hit is None else hit | m
            picks.append(jnp.where(hit, 1.0, 0.0).astype(BF16))
        pick = jnp.concatenate(picks, axis=1)
        xs[here, :] = dot(pick, xgy[0]).astype(BF16)
        gys[here, :] = dot(pick, xgy[1]).astype(BF16)
        mrow[here, :] = dot(pick, mt[...]).astype(BF16)
        os_[here, :] = jnp.zeros((GATHER, DIM), BF16)
        ps[here, :] = jnp.zeros((GATHER, DIM + BLK), BF16)
        gcol[here, :] = jnp.zeros((GATHER, 1), F32)
        return carry

    lax.fori_loop(0, 2 * n_comb, gather, 0)

    def chunks(size, items, left=None):
        lane = lax.broadcasted_iota(I32, (size, BLK), 1)
        heres = [pl.ds(pl.multiple_of(base, 16), size) for _, base, _, _ in items]
        xv = [xs[h, :] for h in heres]
        uv = [dot(x, wgu[it[2]]) for x, it in zip(xv, items)]
        gy = [gys[h, :].astype(F32) for h in heres]
        ms = [mrow[h, :].astype(F32) for h in heres]
        match = [(lane < 3 * TOP_K) & (pltpu.roll(m, BLK - 16, 1) == it[0].astype(F32)) for m, it in zip(ms, items)]
        g = [jnp.sum(jnp.where(k, m, 0.0), axis=1, keepdims=True) for k, m in zip(match, ms)]
        q = [(a * b).astype(BF16) for a, b in zip(g, gy)]
        r = [dot(a, wd[it[2]], ((1,), (1,))) for a, it in zip(q, items)]
        u = [a[:, :DIM].astype(BF16).astype(F32) for a in uv]
        v = [a[:, DIM:].astype(BF16).astype(F32) for a in uv]
        s = [jax.nn.sigmoid(a) for a in u]
        act = [(a * b * c).astype(BF16) for a, b, c in zip(u, s, v)]
        o = [dot(a, wd[it[2]]).astype(BF16) for a, it in zip(act, items)]
        dv = [(a * b * c).astype(BF16) for a, b, c in zip(r, u, s)]
        du = [(a * b * c * (1.0 + d * (1.0 - c))).astype(BF16) for a, b, c, d in zip(r, v, s, u)]
        duv = [jnp.concatenate([a, b], axis=1) for a, b in zip(du, dv)]
        p = [dot(a, wgu[it[2]], ((1,), (1,))).astype(BF16) for a, it in zip(duv, items)]
        for i, h in enumerate(heres):
            dgate = jnp.sum(gy[i] * o[i].astype(F32), axis=1, keepdims=True)
            hi, mid, low = three_parts(dgate)
            spread = jnp.where(lane < TOP_K, hi, jnp.where(lane < 2 * TOP_K, mid, low))
            pd = jnp.concatenate([p[i], jnp.where(match[i], spread, 0.0).astype(BF16)], axis=1)
            if left is None:
                os_[h, :] = o[i]
                ps[h, :] = pd
                gcol[h, :] = g[i]
            else:
                keep = lax.broadcasted_iota(I32, (size, 1), 0) < left
                os_[h, :] = jnp.where(keep, o[i].astype(F32), os_[h, :].astype(F32)).astype(BF16)
                ps[h, :] = jnp.where(keep, pd.astype(F32), ps[h, :].astype(F32)).astype(BF16)
                gcol[h, :] = jnp.where(keep, g[i], gcol[h, :])
            stage = items[i][3]
            stage[:, 0:DIM] = xv[i]
            stage[:, DIM:2 * DIM] = act[i]
            stage[:, 2 * DIM:3 * DIM] = q[i]
            stage[:, 3 * DIM:5 * DIM] = duv[i]

    def small_out(e):
        buf = lax.rem(e, 4)
        return pltpu.make_async_copy(stage_s.at[buf], rows_hbm.at[e, pl.ds(0, SMALL)], s_sem.at[buf])

    def big_out(e, b):
        return pltpu.make_async_copy(stage_b, rows_hbm.at[e, pl.ds(pl.multiple_of(SMALL + b * BIG, 32), BIG)], b_sem)

    def pair(i, sent):
        both = [2 * i, 2 * i + 1]
        for e in both:
            for c in weights(e):
                c.wait()

        @pl.when(i >= 2)
        def _():
            for e in both:
                small_out(e - 4).wait()

        chunks(SMALL, [(e, off_s[e], lax.rem(e, RING), stage_s.at[lax.rem(e, 4)]) for e in both])
        for e in both:
            small_out(e).start()
        for e in both:
            def big(b, n, e=e):
                @pl.when(n > 0)
                def _():
                    big_out(e, b).wait()

                base = SMALL + b * BIG
                chunks(BIG, [(e, off_s[e] + base, lax.rem(e, RING), stage_b)], cnt_ref[e] - base)
                big_out(e, b).start()
                return n + 1

            sent = lax.fori_loop(0, (jnp.maximum(cnt_ref[e] - SMALL, 0) + BIG - 1) // BIG, big, sent)

        @pl.when(i + 2 < LOC // 2)
        def _():
            for e in both:
                for c in weights(e + RING):
                    c.start()

        return sent

    sent = lax.fori_loop(0, LOC // 2, pair, jnp.int32(0))
    for e in range(4):
        small_out(jnp.int32(e)).wait()

    @pl.when(sent > 0)
    def _():
        big_out(jnp.int32(0), 0).wait()

    def leave(n, start):
        r, c, k = n // 4, (n // 2) % 2, n % 2
        dr, dc = lax.rem(row + r, 2), lax.rem(col + c, 2)
        for far in range(2):
            ys, dxs = (keep_y, keep_dx) if far == 0 else (send_y, send_dx)

            @pl.when(lax.rem(core + k, 2) == far)
            def _():
                pltpu.make_async_copy(sy.at[n], ys.at[dc * 2 + dr], out_sem.at[n, 0]).start()
                pltpu.make_async_copy(sdx.at[n], dxs.at[dr * 2 + dc], out_sem.at[n, 1]).start()

    def combine(i, last):
        r0 = pl.multiple_of(i * COMB, COMB)
        here = pl.ds(r0, COMB)
        hi, mid, low = three_parts(gcol[here, :] * os_[here, :].astype(F32))
        tri[0:COMB, :] = hi.astype(BF16)
        tri[COMB:2 * COMB, :] = mid.astype(BF16)
        tri[2 * COMB:, :] = low.astype(BF16)
        rid = (r0 + lax.broadcasted_iota(I32, (1, COMB), 1)).astype(F32)
        for t in range(TOK // 256):
            toks = slice(t * 256, (t + 1) * 256)
            hit = None
            for j in range(TOP_K):
                m = pos_t[toks, 32 + j:33 + j] == rid
                hit = m if hit is None else hit | m
            pick = jnp.where(hit, 1.0, 0.0).astype(BF16)
            yb = dot(jnp.concatenate([pick] * 3, axis=1), tri[...])
            db = dot(pick, ps[here, :])
            for k in range(2):
                n = 2 * t + k
                half = slice(k * BLK, (k + 1) * BLK)
                sy[n, 0:BLK, :] += yb[half]
                sdx[n, :, :] += db[half, :DIM]
                dacc[n, :, :] += db[half, DIM:]
                if last:
                    dgt = dacc[n, :, :].T
                    sy[n, BLK:BLK + TOP_K, 0:BLK] = (dgt[0:TOP_K] + dgt[TOP_K:2 * TOP_K]) + dgt[2 * TOP_K:3 * TOP_K]
                    leave(n, True)

    def combine_step(i, carry):
        combine(i, False)
        return carry

    lax.fori_loop(0, n_comb - 1, combine_step, 0)
    combine(n_comb - 1, True)
    for n in range(N_DEV):
        pltpu.make_async_copy(sy.at[n], keep_y.at[0], out_sem.at[n, 0]).wait()
        pltpu.make_async_copy(sdx.at[n], keep_dx.at[0], out_sem.at[n, 1]).wait()


def run_experts(meta_all, xg, w_gate, w_up, w_down):
    vmem = pl.BlockSpec(memory_space=pltpu.VMEM)
    hbm = pl.BlockSpec(memory_space=pl.ANY)
    y_sum = jax.ShapeDtypeStruct((4, BLK + 8, DIM), F32)
    dx_sum = jax.ShapeDtypeStruct((4, BLK, DIM), F32)
    return pl.pallas_call(
        expert_kernel,
        out_shape=(y_sum, y_sum, dx_sum, dx_sum, jax.ShapeDtypeStruct((LOC, SLAB, 5 * DIM), BF16), jax.ShapeDtypeStruct((LOC,), I32)),
        in_specs=[vmem, hbm, hbm, hbm, hbm],
        out_specs=(hbm, hbm, hbm, hbm, hbm, pl.BlockSpec(memory_space=pltpu.SMEM)),
        scratch_shapes=[
            pltpu.VMEM((2, TOK, DIM), BF16), pltpu.VMEM((TOK, BLK), BF16),
            pltpu.VMEM((RING, DIM, 2 * DIM), BF16), pltpu.VMEM((RING, DIM, DIM), BF16),
            pltpu.VMEM((ROWS, DIM), BF16), pltpu.VMEM((ROWS, DIM), BF16), pltpu.VMEM((ROWS, BLK), BF16),
            pltpu.VMEM((ROWS, DIM), BF16), pltpu.VMEM((ROWS, DIM + BLK), BF16), pltpu.VMEM((ROWS, 1), F32),
            pltpu.VMEM((8, TOK), F32), pltpu.VMEM((TOK, BLK), F32), pltpu.VMEM((3 * COMB, DIM), BF16),
            pltpu.VMEM((N_DEV, BLK + 8, DIM), F32), pltpu.VMEM((N_DEV, BLK, DIM), F32), pltpu.VMEM((N_DEV, BLK, BLK), F32),
            pltpu.SMEM((LOC,), I32),
            pltpu.VMEM((4, SMALL, 5 * DIM), BF16), pltpu.VMEM((BIG, 5 * DIM), BF16),
            pltpu.SemaphoreType.DMA((2,)), pltpu.SemaphoreType.DMA((RING, 3)), pltpu.SemaphoreType.DMA((4,)), pltpu.SemaphoreType.DMA,
            pltpu.SemaphoreType.DMA((N_DEV, 2)),
        ],
        compiler_params=pltpu.CompilerParams(vmem_limit_bytes=VMEM_MAX),
        cost_estimate=pl.CostEstimate(flops=6_000_000_000, bytes_accessed=60_000_000, transcendentals=0),
        name="expert_rows",
    )(meta_all, xg, w_gate, w_up, w_down)


def wgrad_kernel(lo, hi, n_alias, cnt_ref, rows_hbm, *refs):
    gg_hbm, gu_hbm, gd_hbm = refs[n_alias:n_alias + 3]
    small, big, out_gu, out_d, r_sem, b_sem, o_sem = refs[n_alias + 3:]

    def rows_in(i):
        return pltpu.make_async_copy(rows_hbm.at[lo + i, pl.ds(0, SMALL)], small.at[lax.rem(i, 2)], r_sem.at[lax.rem(i, 2)])

    def piece_in(i, b):
        return pltpu.make_async_copy(rows_hbm.at[lo + i, pl.ds(pl.multiple_of(b * PIECE, PIECE), PIECE)], big.at[lax.rem(i, 2)], b_sem.at[lax.rem(i, 2)])

    def fetch(i):
        many = cnt_ref[lo + i] > SMALL

        @pl.when(many)
        def _():
            piece_in(i, 0).start()

        @pl.when(jnp.logical_not(many))
        def _():
            rows_in(i).start()

    def results(i):
        slot, e = lax.rem(i, 2), lo + i
        return (pltpu.make_async_copy(out_gu.at[slot, :, pl.ds(0, DIM)], gg_hbm.at[e], o_sem.at[slot, 0]),
                pltpu.make_async_copy(out_gu.at[slot, :, pl.ds(DIM, DIM)], gu_hbm.at[e], o_sem.at[slot, 1]),
                pltpu.make_async_copy(out_d.at[slot], gd_hbm.at[e], o_sem.at[slot, 2]))

    def products(ref, size, left):
        keep = lax.broadcasted_iota(I32, (size, 1), 0) < left
        part = lambda a, b: jnp.where(keep, ref[:, a * DIM:b * DIM].astype(F32), 0.0).astype(BF16)
        x, a, q, duv = part(0, 1), part(1, 2), part(2, 3), part(3, 5)
        return dot(x, duv, ((0,), (0,))), dot(a, q, ((0,), (0,)))

    fetch(jnp.int32(0))

    def expert(i, carry):
        slot = lax.rem(i, 2)
        cnt = cnt_ref[lo + i]

        @pl.when(i + 1 < hi - lo)
        def _():
            fetch(i + 1)

        @pl.when(i >= 2)
        def _():
            for c in results(i - 2):
                c.wait()

        @pl.when(cnt <= SMALL)
        def _():
            rows_in(i).wait()
            g1, g2 = products(small.at[slot], SMALL, cnt)
            out_gu[slot] = g1
            out_d[slot] = g2

        @pl.when(cnt > SMALL)
        def _():
            piece_in(i, 0).wait()
            g1, g2 = products(big.at[slot], PIECE, cnt)
            out_gu[slot] = g1
            out_d[slot] = g2

            def more(b, c2):
                piece_in(i, b).start()
                piece_in(i, b).wait()
                g1, g2 = products(big.at[slot], PIECE, cnt - b * PIECE)
                out_gu[slot] += g1
                out_d[slot] += g2
                return c2

            lax.fori_loop(1, (cnt + PIECE - 1) // PIECE, more, 0)

        for c in results(i):
            c.start()
        return carry

    lax.fori_loop(0, hi - lo, expert, 0)
    for i in (hi - lo - 2, hi - lo - 1):
        for c in results(jnp.int32(i)):
            c.wait()


def weight_grads(lo, hi, cnt, rows, earlier=()):
    hbm = pl.BlockSpec(memory_space=pl.ANY)
    out = jax.ShapeDtypeStruct((LOC, DIM, DIM), F32)
    return pl.pallas_call(
        functools.partial(wgrad_kernel, lo, hi, len(earlier)),
        out_shape=(out, out, out),
        in_specs=[pl.BlockSpec(memory_space=pltpu.SMEM), hbm] + [hbm] * len(earlier),
        out_specs=(hbm, hbm, hbm),
        input_output_aliases={2 + i: i for i in range(len(earlier))},
        scratch_shapes=[
            pltpu.VMEM((2, SMALL, 5 * DIM), BF16), pltpu.VMEM((2, PIECE, 5 * DIM), BF16),
            pltpu.VMEM((2, DIM, 2 * DIM), F32), pltpu.VMEM((2, DIM, DIM), F32),
            pltpu.SemaphoreType.DMA((2,)), pltpu.SemaphoreType.DMA((2,)), pltpu.SemaphoreType.DMA((2, 3)),
        ],
        compiler_params=pltpu.CompilerParams(vmem_limit_bytes=36 * 1024 * 1024),
        cost_estimate=pl.CostEstimate(flops=(hi - lo) * 400_000_000, bytes_accessed=(hi - lo) * 5_000_000, transcendentals=0),
        name="weight_grads",
    )(cnt, rows, *earlier)


def solution(mesh):
    tok_spec = P(None, ALL_AXES, None)
    w_spec = P(ALL_AXES, None, None)

    def swap(value, axis):
        return lax.ppermute(value, axis, [(0, 1), (1, 0)])

    def moe_layer(x, route_idx, gates, w_gate, w_up, w_down, grad_y):
        tok_dev = x.shape[1]
        flat = lambda a: a.reshape(2 * tok_dev, -1)
        turn = lambda a: jnp.transpose(a, (0, 2, 1))
        xg, meta_all = all_gather_tokens(flat(x), flat(grad_y), turn(route_idx), turn(gates))
        keep_y, send_y, keep_dx, send_dx, rows, cnt = run_experts(meta_all, xg.reshape(2, TOK, DIM), w_gate, w_up, w_down)
        chip_y = keep_y + swap(send_y, "core")
        chip_dx = keep_dx + swap(send_dx, "core")
        y_in = swap(chip_y[2:], "col")
        dx_in = swap(chip_dx[2:], "row")
        early = weight_grads(0, 10, cnt, rows)
        y_far = swap(chip_y[1] + y_in[1], "row")
        dx_far = swap(chip_dx[1] + dx_in[1], "col")
        g_gate, g_up, g_down = weight_grads(10, LOC, cnt, rows, early)
        y_sum = chip_y[0] + y_in[0] + y_far
        dx_sum = chip_dx[0] + dx_in[0] + dx_far
        y = y_sum[:BLK].astype(BF16).reshape(x.shape)
        dx = dx_sum.astype(BF16).reshape(x.shape)
        dg = turn(jnp.stack([y_sum[BLK:BLK + TOP_K, m * tok_dev:(m + 1) * tok_dev] for m in range(2)]))
        return y, dx, dg, g_gate, g_up, g_down

    return jax.shard_map(moe_layer, mesh=mesh, in_specs=(tok_spec, tok_spec, tok_spec, w_spec, w_spec, w_spec, tok_spec), out_specs=(tok_spec, tok_spec, tok_spec, w_spec, w_spec, w_spec), check_vma=False)
```

time: 114 us -> 104 us (0.912)
  starting transfers between devices: 16.5 us -> 4.88 us
  local copies, waits for them, and re-layouts: 5.33 us -> 0.86 us
  Pallas kernels: 87.9 us -> 91.8 us
  waiting for transfers between devices: 0.97 us -> 2.93 us
    ppermute x6, starting transfers between devices: 16.5 us -> 4.88 us  [swap(): return lax.ppermute(value, axis, [(0, 1), (1, 0)])]
    pallas_call x2, Pallas kernels: 57.1 us -> 60.1 us  [the longest x1 40.9 us: run_experts(): pl.pallas_call(expert_kernel, out_shape=(y_sum, y_sum, dx_sum, dx_sum, ja...]
    squeeze x2 -> x0, local copies, waits for them, and re-layouts: 3 us -> none  [the longest x1 1.58 us: moe_layer(): chip_y = sum_y[0] + swap(sum_y[1], 'core')]
    ppermute x6, waiting for transfers between devices: 0.97 us -> 2.93 us  [swap(): return lax.ppermute(value, axis, [(0, 1), (1, 0)])]
    add x3, other arithmetic: 0.34 us -> 1.79 us  [the longest x1 1.61 us: moe_layer(): chip_dx = keep_dx + swap(send_dx, 'core')]
    unnamed x8 -> x4, local copies, waits for them, and re-layouts: 1.3 us -> 0.01 us
  transfers between devices with their start and end apart: 6 -> 6, of which waited for: 1 -> 2; matrix products, arithmetic and copies ran while one was open for 2% -> 3% of each run, Pallas kernels for 27% -> 30%
where the time goes in v2:
time: 104 us
  Pallas kernels  91.8 us (88%)
  starting transfers between devices  4.88 us (5%)
  other arithmetic  3.2 us (3%)
  waiting for transfers between devices  2.93 us (3%)
    pallas_call x1, Pallas kernels, run_experts(): pl.pallas_call(expert_kernel, out_shape=(y_sum, y_sum, dx_sum, dx_sum, ja...  40.9 us
    pallas_call x2, Pallas kernels, weight_grads(): pl.pallas_call(functools.partial(wgrad_kernel, lo, hi, len(earlier)), out...  31.7 us
    pallas_call x1, Pallas kernels, all_gather_tokens(): pl.pallas_call(gather_kernel, out_shape=(jax.ShapeDtypeStruct((2, N_DEV,...  19.2 us
    ppermute x6, starting transfers between devices, swap(): return lax.ppermute(value, axis, [(0, 1), (1, 0)])  4.88 us
    ppermute x6, waiting for transfers between devices, swap(): return lax.ppermute(value, axis, [(0, 1), (1, 0)])  2.93 us
  transfers between devices with their start and end apart: 6, of which 2 were waited for; matrix products, arithmetic and copies ran while one was open for 3% of the time, Pallas kernels for 30%

profile of v2, /device:TPU:0, one launch (start us, length us, event | category | flops | bytes accessed | tf_op | source)
XLA Modules:
  0.0 104.4 jit_solution(1638659684111057204)
XLA Ops:
  0.6 19.2 %token_gather.1 = (bf16[2,8,128,640]{3,2,1,0:T(8,128)(2,1)}, f32[8,8,128]{2,1,0:T(8,128)}) custom-call(bf16[128,640]{1,0:T(8,128)(2,1)} %bitcast.29, bf16[128,640]{1,0:T(8,128)(2,1)} %bitcast.30, s32[2,4,64]{2,1,0:T(4,128)} %bitcast.32, f32[2,4,64]{2,1,0:T(4,128)} %bitcast.33), custom_call_target="tpu_custom_call" | custom-call | tf_op jit(solution)/shard_map/token_gather/pallas_call | solution.py:138
  19.8 40.9 %expert_rows.1 = (f32[4,136,640]{2,1,0:T(8,128)}, f32[4,136,640]{2,1,0:T(8,128)}, f32[4,128,640]{2,1,0:T(8,128)}, f32[4,128,640]{2,1,0:T(8,128)}, bf16[16,640,3200]{2,1,0:T(8,128)(2,1)}, /*index=5*/s32[16]{0:T(128)}) custom-call(f32[8,8,128]{2,1,0:T(8,128)} %get-tuple-element.20.meta_ref, bf16[2,1024,640]{2,1,0:T(8,128)(2,1)} %bitcast.27, ...), custom_call_target="tpu_custom_call" | custom-call | flops 6000000000 | bytes 60000000 | tf_op jit(solution)/shard_map/expert_rows/pallas_call | solution.py:390
  60.7 1.0 collective-permute-start.3
  61.8 0.0 collective-permute-start
  61.8 2.6 %collective-permute-done.3 = f32[4,128,640]{2,1,0:T(8,128)S(1)} collective-permute-done((f32[4,128,640]{2,1,0:T(8,128)}, f32[4,128,640]{2,1,0:T(8,128)S(1)}, u32[]{:S(2)}, u32[]{:S(2)}) %collective-permute-start.3) | collective-permute-done | bytes 1310752 | tf_op jit(solution)/shard_map/ppermute | solution.py:520
  64.4 0.0 copy-start.1
  64.4 1.6 %add.42 = f32[4,128,640]{2,1,0:T(8,128)S(1)} add(f32[4,128,640]{2,1,0:T(8,128)} %get-tuple-element.24, f32[4,128,640]{2,1,0:T(8,128)S(1)} %collective-permute-done.3) | non-fusion elementwise | flops 327680 | bytes 3932160 | tf_op jit(solution)/shard_map/add | solution.py:529
  66.1 0.0 collective-permute-start.4
  66.1 0.3 collective-permute-done
  66.4 0.0 copy-done.1
  66.4 0.1 add.36
  66.6 0.0 copy-start
  66.6 1.7 %collective-permute-start.1 = (f32[2,136,640]{2,1,0:T(8,128)S(1)}, f32[2,136,640]{2,1,0:T(8,128)S(1)}, u32[]{:S(2)}, u32[]{:S(2)}) collective-permute-start(f32[2,136,640]{2,1,0:T(8,128)S(1)} %slice.54), channel_id=1, source_target_pairs={{0,2},{2,0},{1,3},{3,1},{4,6},{6,4},{5,7},{7,5}} | collective-permute-start | bytes 2088968 | tf_op jit(solution)/shard_map/ppermute | solution.py:520
  68.4 0.0 copy-done
  68.4 19.6 %weight_grads.2 = (f32[16,640,640]{2,1,0:T(8,128)}, f32[16,640,640]{2,1,0:T(8,128)}, f32[16,640,640]{2,1,0:T(8,128)}) custom-call(s32[16]{0:T(128)S(1)} %copy-done, bf16[16,640,3200]{2,1,0:T(8,128)(2,1)} %get-tuple-element.27.rows_hbm), custom_call_target="tpu_custom_call" | custom-call | flops 4000000000 | bytes 50000000 | tf_op jit(solution)/shard_map/weight_grads/pallas_call | solution.py:498
  88.0 0.0 collective-permute-done.4
  88.0 0.0 collective-permute-start.5
  88.1 0.0 collective-permute-done.1
  88.1 2.0 %collective-permute-start.2 = (f32[136,640]{1,0:T(8,128)S(1)}, f32[136,640]{1,0:T(8,128)S(1)}, u32[]{:S(2)}, u32[]{:S(2)}) collective-permute-start(f32[136,640]{1,0:T(8,128)S(1)} %fusion), channel_id=1, source_target_pairs={{0,4},{4,0},{1,5},{5,1},{2,6},{6,2},{3,7},{7,3}} | collective-permute-start | bytes 1044488 | tf_op jit(solution)/shard_map/ppermute | solution.py:520
  90.1 12.1 %weight_grads.3 = (f32[16,640,640]{2,1,0:T(8,128)}, f32[16,640,640]{2,1,0:T(8,128)}, f32[16,640,640]{2,1,0:T(8,128)}) custom-call(s32[16]{0:T(128)S(1)} %copy-done, bf16[16,640,3200]{2,1,0:T(8,128)(2,1)} %get-tuple-element.27.rows_hbm, f32[16,640,640]{2,1,0:T(8,128)} %get-tuple-element.28.refs_0_, ...), custom_call_target="tpu_custom_call", output_to_operand_aliasing={{0}: (2, {}), {1}: (3, {}), {2}: (4, {})} | custom-call | flops 2400000000 | bytes 30000000 | tf_op jit(solution)/shard_map/weight_grads/pallas_call | solution.py:498
  102.3 0.0 collective-permute-done.5
  102.3 0.7 fusion.6
  103.0 0.0 collective-permute-done.2
  103.0 0.1 fusion.2
  103.1 0.1 slice_bitcast_fusion.1
  103.1 0.7 slice.91
  103.8 0.6 maximum_bitcast_fusion
  (4 shorter events, 0.2 us)
Async XLA Ops:
  60.7 3.7 %collective-permute-start.3 = (f32[4,128,640]{2,1,0:T(8,128)}, f32[4,128,640]{2,1,0:T(8,128)S(1)}, u32[]{:S(2)}, u32[]{:S(2)}) collective-permute-start(f32[4,128,640]{2,1,0:T(8,128)} %get-tuple-element.25), channel_id=1, source_target_pairs={{0,1},{1,0},{2,3},{3,2},{4,5},{5,4},{6,7},{7,6}} | collective-permute-start | bytes 3932168 | tf_op jit(solution)/shard_map/ppermute | solution.py:520
  61.8 4.7 %collective-permute-start = (f32[4,136,640]{2,1,0:T(8,128)}, f32[4,136,640]{2,1,0:T(8,128)S(1)}, u32[]{:S(2)}, u32[]{:S(2)}) collective-permute-start(f32[4,136,640]{2,1,0:T(8,128)} %get-tuple-element.23), channel_id=1, source_target_pairs={{0,1},{1,0},{2,3},{3,2},{4,5},{5,4},{6,7},{7,6}} | collective-permute-start | bytes 4177928 | tf_op jit(solution)/shard_map/ppermute | solution.py:520
  64.4 2.0 %copy-start.1 = (f32[4,136,640]{2,1,0:T(8,128)S(1)}, f32[4,136,640]{2,1,0:T(8,128)}, u32[]{:S(2)}) copy-start(f32[4,136,640]{2,1,0:T(8,128)} %get-tuple-element.22) | copy-start | bytes 4177924
  66.1 21.9 %collective-permute-start.4 = (f32[2,128,640]{2,1,0:T(8,128)S(1)}, f32[2,128,640]{2,1,0:T(8,128)S(1)}, u32[]{:S(2)}, u32[]{:S(2)}) collective-permute-start(f32[2,128,640]{2,1,0:T(8,128)S(1)} %slice.60), channel_id=1, source_target_pairs={{0,4},{4,0},{1,5},{5,1},{2,6},{6,2},{3,7},{7,3}} | collective-permute-start | bytes 1966088 | tf_op jit(solution)/shard_map/ppermute | solution.py:520
  66.6 1.8 %copy-start = (s32[16]{0:T(128)S(1)}, s32[16]{0:T(128)}, u32[]{:S(2)}) copy-start(s32[16]{0:T(128)} %get-tuple-element.26.cnt_ref) | copy-start | bytes 196
  66.6 21.4 %collective-permute-start.1 = (f32[2,136,640]{2,1,0:T(8,128)S(1)}, f32[2,136,640]{2,1,0:T(8,128)S(1)}, u32[]{:S(2)}, u32[]{:S(2)}) collective-permute-start(f32[2,136,640]{2,1,0:T(8,128)S(1)} %slice.54), channel_id=1, source_target_pairs={{0,2},{2,0},{1,3},{3,1},{4,6},{6,4},{5,7},{7,5}} | collective-permute-start | bytes 2088968 | tf_op jit(solution)/shard_map/ppermute | solution.py:520
  88.0 14.2 %collective-permute-start.5 = (f32[128,640]{1,0:T(8,128)S(1)}, f32[128,640]{1,0:T(8,128)S(1)}, u32[]{:S(2)}, u32[]{:S(2)}) collective-permute-start(f32[128,640]{1,0:T(8,128)S(1)} %fusion.3), channel_id=1, source_target_pairs={{0,2},{2,0},{1,3},{3,1},{4,6},{6,4},{5,7},{7,5}} | collective-permute-start | bytes 983048 | tf_op jit(solution)/shard_map/ppermute | solution.py:520
  88.1 14.9 %collective-permute-start.2 = (f32[136,640]{1,0:T(8,128)S(1)}, f32[136,640]{1,0:T(8,128)S(1)}, u32[]{:S(2)}, u32[]{:S(2)}) collective-permute-start(f32[136,640]{1,0:T(8,128)S(1)} %fusion), channel_id=1, source_target_pairs={{0,4},{4,0},{1,5},{5,1},{2,6},{6,2},{3,7},{7,3}} | collective-permute-start | bytes 1044488 | tf_op jit(solution)/shard_map/ppermute | solution.py:520

commit v3 on v2

--- a/solution.py
+++ b/solution.py
@@ -21,7 +21,7 @@
 GATHER = 128
 COMB = 256
 SMALL, BIG = 32, 256
-ROWS = 4864
+ROWS = 4640
 SLAB = 640
 RING = 4
 PIECE = 288
@@ -154,16 +154,17 @@
     return hi, mid, value - hi - mid
 
 
-def expert_kernel(meta_ref, xg_hbm, wg_hbm, wu_hbm, wd_hbm, keep_y, send_y, keep_dx, send_dx, rows_hbm, cnt_ref,
+def expert_kernel(meta_ref, xg_hbm, wg_hbm, wu_hbm, wd_hbm, near_k, near_s, far_k, far_s, rows_hbm, cnt_ref,
                   xgy, mt, wgu, wd, xs, gys, mrow, os_, ps, gcol, pos, pos_t, tri, sy, sdx, dacc, off_s, stage_s, stage_b,
                   x_sem, w_sem, s_sem, b_sem, out_sem):
     row, col, core = (lax.axis_index(a) for a in GROUP_AXES)
     first = ((row * 2 + col) * 2 + core) * LOC
+    sums = ((near_k, near_s), (far_k, far_s))
 
     def weights(e):
-        slot = lax.rem(e, RING)
-        return (pltpu.make_async_copy(wg_hbm.at[e], wgu.at[slot, :, pl.ds(0, DIM)], w_sem.at[slot, 0]),
-                pltpu.make_async_copy(wu_hbm.at[e], wgu.at[slot, :, pl.ds(DIM, DIM)], w_sem.at[slot, 1]),
+        slot, wide = lax.rem(e, RING), lax.rem(e, RING + 2)
+        return (pltpu.make_async_copy(wg_hbm.at[e], wgu.at[wide, :, pl.ds(0, DIM)], w_sem.at[slot, 0]),
+                pltpu.make_async_copy(wu_hbm.at[e], wgu.at[wide, :, pl.ds(DIM, DIM)], w_sem.at[slot, 1]),
                 pltpu.make_async_copy(wd_hbm.at[e], wd.at[slot], w_sem.at[slot, 2]))
 
     tokens_in = [pltpu.make_async_copy(xg_hbm.at[h], xgy.at[h], x_sem.at[h]) for h in range(2)]
@@ -242,45 +243,74 @@
 
     lax.fori_loop(0, 2 * n_comb, gather, 0)
 
-    def chunks(size, items, left=None):
+    def chunks(size, items, left=None, between=iter(())):
         lane = lax.broadcasted_iota(I32, (size, BLK), 1)
-        heres = [pl.ds(pl.multiple_of(base, 16), size) for _, base, _, _ in items]
+        heres = [pl.ds(pl.multiple_of(it[1], 16), size) for it in items]
         xv = [xs[h, :] for h in heres]
-        uv = [dot(x, wgu[it[2]]) for x, it in zip(xv, items)]
+        credit = [0.0]
+
+        def tiled(width, cost, product):
+            tiles = []
+            for n in range(0, width, 256):
+                m = min(n + 256, width)
+                tiles.append(product(n, m))
+                credit[0] += cost * (m - n) / 256
+                while credit[0] >= 1.0:
+                    next(between, None)
+                    credit[0] -= 1.0
+            return jnp.concatenate(tiles, axis=1)
+
+        uv = [tiled(2 * DIM, 0.36, lambda n, m, x=x, it=it: dot(x, wgu[it[3], :, n:m])) for x, it in zip(xv, items)]
         gy = [gys[h, :].astype(F32) for h in heres]
         ms = [mrow[h, :].astype(F32) for h in heres]
         match = [(lane < 3 * TOP_K) & (pltpu.roll(m, BLK - 16, 1) == it[0].astype(F32)) for m, it in zip(ms, items)]
         g = [jnp.sum(jnp.where(k, m, 0.0), axis=1, keepdims=True) for k, m in zip(match, ms)]
         q = [(a * b).astype(BF16) for a, b in zip(g, gy)]
-        r = [dot(a, wd[it[2]], ((1,), (1,))) for a, it in zip(q, items)]
+        r = [tiled(DIM, 0.85, lambda n, m, a=a, it=it: dot(a, wd[it[2], n:m, :], ((1,), (1,)))) for a, it in zip(q, items)]
         u = [a[:, :DIM].astype(BF16).astype(F32) for a in uv]
         v = [a[:, DIM:].astype(BF16).astype(F32) for a in uv]
         s = [jax.nn.sigmoid(a) for a in u]
         act = [(a * b * c).astype(BF16) for a, b, c in zip(u, s, v)]
-        o = [dot(a, wd[it[2]]).astype(BF16) for a, it in zip(act, items)]
+        o = [tiled(DIM, 0.43, lambda n, m, a=a, it=it: dot(a, wd[it[2], :, n:m])).astype(BF16) for a, it in zip(act, items)]
         dv = [(a * b * c).astype(BF16) for a, b, c in zip(r, u, s)]
         du = [(a * b * c * (1.0 + d * (1.0 - c))).astype(BF16) for a, b, c, d in zip(r, v, s, u)]
         duv = [jnp.concatenate([a, b], axis=1) for a, b in zip(du, dv)]
-        p = [dot(a, wgu[it[2]], ((1,), (1,))).astype(BF16) for a, it in zip(duv, items)]
         for i, h in enumerate(heres):
             dgate = jnp.sum(gy[i] * o[i].astype(F32), axis=1, keepdims=True)
             hi, mid, low = three_parts(dgate)
             spread = jnp.where(lane < TOP_K, hi, jnp.where(lane < 2 * TOP_K, mid, low))
-            pd = jnp.concatenate([p[i], jnp.where(match[i], spread, 0.0).astype(BF16)], axis=1)
+            dgs = jnp.where(match[i], spread, 0.0).astype(BF16)
             if left is None:
                 os_[h, :] = o[i]
-                ps[h, :] = pd
+                ps[h, DIM:] = dgs
                 gcol[h, :] = g[i]
             else:
+                p = dot(duv[i], wgu[items[i][3]], ((1,), (1,))).astype(BF16)
+                pd = jnp.concatenate([p, dgs], axis=1)
                 keep = lax.broadcasted_iota(I32, (size, 1), 0) < left
                 os_[h, :] = jnp.where(keep, o[i].astype(F32), os_[h, :].astype(F32)).astype(BF16)
                 ps[h, :] = jnp.where(keep, pd.astype(F32), ps[h, :].astype(F32)).astype(BF16)
                 gcol[h, :] = jnp.where(keep, g[i], gcol[h, :])
-            stage = items[i][3]
+            stage = items[i][4]
             stage[:, 0:DIM] = xv[i]
             stage[:, DIM:2 * DIM] = act[i]
             stage[:, 2 * DIM:3 * DIM] = q[i]
             stage[:, 3 * DIM:5 * DIM] = duv[i]
+
+    def input_grads(items):
+        for _, base, _, wide, stage in items:
+            duv = stage[:, 3 * DIM:5 * DIM]
+            for d in range(0, DIM, 128):
+                p = dot(wgu[wide, d:d + 128, :], duv, ((1,), (1,))).T.astype(BF16)
+                ps[pl.ds(pl.multiple_of(base, 16), SMALL), d:d + 128] = p
+                yield
+
+    def small(e):
+        return (e, off_s[e], lax.rem(e, RING), lax.rem(e, RING + 2), stage_s.at[lax.rem(e, 4)])
+
+    def earlier(e, i):
+        before = lax.rem(e + LOC - 2, LOC)
+        return (before, jnp.where(i > 0, off_s[before], ROWS - SMALL), 0, lax.rem(e + RING, RING + 2), stage_s.at[lax.rem(e + 2, 4)])
 
     def small_out(e):
         buf = lax.rem(e, 4)
@@ -300,7 +330,10 @@
             for e in both:
                 small_out(e - 4).wait()
 
-        chunks(SMALL, [(e, off_s[e], lax.rem(e, RING), stage_s.at[lax.rem(e, 4)]) for e in both])
+        between = input_grads([earlier(e, i) for e in both])
+        chunks(SMALL, [small(e) for e in both], between=between)
+        for _ in between:
+            pass
         for e in both:
             small_out(e).start()
         for e in both:
@@ -310,7 +343,7 @@
                     big_out(e, b).wait()
 
                 base = SMALL + b * BIG
-                chunks(BIG, [(e, off_s[e] + base, lax.rem(e, RING), stage_b)], cnt_ref[e] - base)
+                chunks(BIG, [(e, off_s[e] + base, lax.rem(e, RING), lax.rem(e, RING + 2), stage_b)], cnt_ref[e] - base)
                 big_out(e, b).start()
                 return n + 1
 
@@ -325,6 +358,8 @@
         return sent
 
     sent = lax.fori_loop(0, LOC // 2, pair, jnp.int32(0))
+    for _ in input_grads([small(jnp.int32(e)) for e in (LOC - 2, LOC - 1)]):
+        pass
     for e in range(4):
         small_out(jnp.int32(e)).wait()
 
@@ -332,16 +367,18 @@
     def _():
         big_out(jnp.int32(0), 0).wait()
 
-    def leave(n, start):
+    def leave(n):
         r, c, k = n // 4, (n // 2) % 2, n % 2
-        dr, dc = lax.rem(row + r, 2), lax.rem(col + c, 2)
+        dr, dc, dk = lax.rem(row + r, 2), lax.rem(col + c, 2), lax.rem(core + k, 2)
         for far in range(2):
-            ys, dxs = (keep_y, keep_dx) if far == 0 else (send_y, send_dx)
-
-            @pl.when(lax.rem(core + k, 2) == far)
-            def _():
-                pltpu.make_async_copy(sy.at[n], ys.at[dc * 2 + dr], out_sem.at[n, 0]).start()
-                pltpu.make_async_copy(sdx.at[n], dxs.at[dr * 2 + dc], out_sem.at[n, 1]).start()
+            for send in range(2):
+                @pl.when((dk == send) & (dc == far))
+                def _():
+                    pltpu.make_async_copy(sy.at[n], sums[far][send].at[dr], out_sem.at[n, 0]).start()
+
+                @pl.when((dk == send) & (dr == far))
+                def _():
+                    pltpu.make_async_copy(sdx.at[n], sums[far][send].at[2 + dc, pl.ds(0, BLK)], out_sem.at[n, 1]).start()
 
     def combine(i, last):
         r0 = pl.multiple_of(i * COMB, COMB)
@@ -369,7 +406,7 @@
                 if last:
                     dgt = dacc[n, :, :].T
                     sy[n, BLK:BLK + TOP_K, 0:BLK] = (dgt[0:TOP_K] + dgt[TOP_K:2 * TOP_K]) + dgt[2 * TOP_K:3 * TOP_K]
-                    leave(n, True)
+                    leave(n)
 
     def combine_step(i, carry):
         combine(i, False)
@@ -378,23 +415,22 @@
     lax.fori_loop(0, n_comb - 1, combine_step, 0)
     combine(n_comb - 1, True)
     for n in range(N_DEV):
-        pltpu.make_async_copy(sy.at[n], keep_y.at[0], out_sem.at[n, 0]).wait()
-        pltpu.make_async_copy(sdx.at[n], keep_dx.at[0], out_sem.at[n, 1]).wait()
+        pltpu.make_async_copy(sy.at[n], near_k.at[0], out_sem.at[n, 0]).wait()
+        pltpu.make_async_copy(sdx.at[n], near_k.at[2, pl.ds(0, BLK)], out_sem.at[n, 1]).wait()
 
 
 def run_experts(meta_all, xg, w_gate, w_up, w_down):
     vmem = pl.BlockSpec(memory_space=pltpu.VMEM)
     hbm = pl.BlockSpec(memory_space=pl.ANY)
-    y_sum = jax.ShapeDtypeStruct((4, BLK + 8, DIM), F32)
-    dx_sum = jax.ShapeDtypeStruct((4, BLK, DIM), F32)
+    sums = jax.ShapeDtypeStruct((4, BLK + 8, DIM), F32)
     return pl.pallas_call(
         expert_kernel,
-        out_shape=(y_sum, y_sum, dx_sum, dx_sum, jax.ShapeDtypeStruct((LOC, SLAB, 5 * DIM), BF16), jax.ShapeDtypeStruct((LOC,), I32)),
+        out_shape=(*[sums] * 4, jax.ShapeDtypeStruct((LOC, SLAB, 5 * DIM), BF16), jax.ShapeDtypeStruct((LOC,), I32)),
         in_specs=[vmem, hbm, hbm, hbm, hbm],
-        out_specs=(hbm, hbm, hbm, hbm, hbm, pl.BlockSpec(memory_space=pltpu.SMEM)),
+        out_specs=(*[hbm] * 5, pl.BlockSpec(memory_space=pltpu.SMEM)),
         scratch_shapes=[
             pltpu.VMEM((2, TOK, DIM), BF16), pltpu.VMEM((TOK, BLK), BF16),
-            pltpu.VMEM((RING, DIM, 2 * DIM), BF16), pltpu.VMEM((RING, DIM, DIM), BF16),
+            pltpu.VMEM((RING + 2, DIM, 2 * DIM), BF16), pltpu.VMEM((RING, DIM, DIM), BF16),
             pltpu.VMEM((ROWS, DIM), BF16), pltpu.VMEM((ROWS, DIM), BF16), pltpu.VMEM((ROWS, BLK), BF16),
             pltpu.VMEM((ROWS, DIM), BF16), pltpu.VMEM((ROWS, DIM + BLK), BF16), pltpu.VMEM((ROWS, 1), F32),
             pltpu.VMEM((8, TOK), F32), pltpu.VMEM((TOK, BLK), F32), pltpu.VMEM((3 * COMB, DIM), BF16),
@@ -524,20 +560,22 @@
         flat = lambda a: a.reshape(2 * tok_dev, -1)
         turn = lambda a: jnp.transpose(a, (0, 2, 1))
         xg, meta_all = all_gather_tokens(flat(x), flat(grad_y), turn(route_idx), turn(gates))
-        keep_y, send_y, keep_dx, send_dx, rows, cnt = run_experts(meta_all, xg.reshape(2, TOK, DIM), w_gate, w_up, w_down)
-        chip_y = keep_y + swap(send_y, "core")
-        chip_dx = keep_dx + swap(send_dx, "core")
-        y_in = swap(chip_y[2:], "col")
-        dx_in = swap(chip_dx[2:], "row")
+        near_k, near_s, far_k, far_s, rows, cnt = run_experts(meta_all, xg.reshape(2, TOK, DIM), w_gate, w_up, w_down)
+        far_in = swap(far_s, "core")
+        y_in = swap(far_k[:2] + far_in[:2], "col")
+        dx_in = swap(far_k[2:, :BLK] + far_in[2:, :BLK], "row")
+        near_in = swap(near_s, "core")
         early = weight_grads(0, 10, cnt, rows)
-        y_far = swap(chip_y[1] + y_in[1], "row")
-        dx_far = swap(chip_dx[1] + dx_in[1], "col")
+        y_out = near_k[1] + near_in[1] + y_in[1]
+        dx_out = near_k[3, :BLK] + near_in[3, :BLK] + dx_in[1]
+        y_out, dx_out, early = lax.optimization_barrier((y_out, dx_out, early))
+        y_far, dx_far = swap(y_out, "row"), swap(dx_out, "col")
         g_gate, g_up, g_down = weight_grads(10, LOC, cnt, rows, early)
-        y_sum = chip_y[0] + y_in[0] + y_far
-        dx_sum = chip_dx[0] + dx_in[0] + dx_far
-        y = y_sum[:BLK].astype(BF16).reshape(x.shape)
-        dx = dx_sum.astype(BF16).reshape(x.shape)
-        dg = turn(jnp.stack([y_sum[BLK:BLK + TOP_K, m * tok_dev:(m + 1) * tok_dev] for m in range(2)]))
+        y = (near_k[0, :BLK] + near_in[0, :BLK] + y_in[0, :BLK] + y_far[:BLK]).astype(BF16).reshape(x.shape)
+        dx = (near_k[2, :BLK] + near_in[2, :BLK] + dx_in[0] + dx_far).astype(BF16).reshape(x.shape)
+        tail = slice(BLK, BLK + TOP_K)
+        dg = near_k[0, tail, :BLK] + near_in[0, tail, :BLK] + y_in[0, tail, :BLK] + y_far[tail, :BLK]
+        dg = turn(jnp.stack([dg[:, m * tok_dev:(m + 1) * tok_dev] for m in range(2)]))
         return y, dx, dg, g_gate, g_up, g_down
 
     return jax.shard_map(moe_layer, mesh=mesh, in_specs=(tok_spec, tok_spec, tok_spec, w_spec, w_spec, w_spec, tok_spec), out_specs=(tok_spec, tok_spec, tok_spec, w_spec, w_spec, w_spec), check_vma=False)

time: 104 us -> 102 us (0.981)
  Pallas kernels: 91.8 us -> 84.2 us
  starting transfers between devices: 4.88 us -> 11.3 us
    ppermute x6, starting transfers between devices: 4.88 us -> 11.3 us  [swap(): return lax.ppermute(value, axis, [(0, 1), (1, 0)])]
    pallas_call x1, Pallas kernels: 40.9 us -> 34.6 us  [run_experts(): pl.pallas_call(expert_kernel, out_shape=(*[sums] * 4, jax.ShapeDtypeStruc...]
    pallas_call x2, Pallas kernels: 31.7 us -> 30.4 us  [weight_grads(): pl.pallas_call(functools.partial(wgrad_kernel, lo, hi, len(earlier)), out...]
  transfers between devices with their start and end apart: 6 -> 6, of which waited for: 2 -> 1; matrix products, arithmetic and copies ran while one was open for 3% -> 2% of each run, Pallas kernels for 30% -> 30%
where the time goes in v3:
time: 102 us
  Pallas kernels  84.2 us (83%)
  starting transfers between devices  11.3 us (11%)
  other arithmetic  2.83 us (3%)
  waiting for transfers between devices  2.76 us (3%)
    pallas_call x1, Pallas kernels, run_experts(): pl.pallas_call(expert_kernel, out_shape=(*[sums] * 4, jax.ShapeDtypeStruc...  34.6 us
    pallas_call x2, Pallas kernels, weight_grads(): pl.pallas_call(functools.partial(wgrad_kernel, lo, hi, len(earlier)), out...  30.4 us
    pallas_call x1, Pallas kernels, all_gather_tokens(): pl.pallas_call(gather_kernel, out_shape=(jax.ShapeDtypeStruct((2, N_DEV,...  19.2 us
    ppermute x6, starting transfers between devices, swap(): return lax.ppermute(value, axis, [(0, 1), (1, 0)])  11.3 us
    ppermute x6, waiting for transfers between devices, swap(): return lax.ppermute(value, axis, [(0, 1), (1, 0)])  2.76 us
  transfers between devices with their start and end apart: 6, of which 1 were waited for; matrix products, arithmetic and copies ran while one was open for 2% of the time, Pallas kernels for 30%

profile of v3, /device:TPU:0, one launch (start us, length us, event | category | flops | bytes accessed | tf_op | source)
XLA Modules:
  0.0 101.9 jit_solution(12467082833987933583)
XLA Ops:
  0.6 19.2 %token_gather.1 = (bf16[2,8,128,640]{3,2,1,0:T(8,128)(2,1)}, f32[8,8,128]{2,1,0:T(8,128)}) custom-call(bf16[128,640]{1,0:T(8,128)(2,1)} %bitcast.34, bf16[128,640]{1,0:T(8,128)(2,1)} %bitcast.35, s32[2,4,64]{2,1,0:T(4,128)} %bitcast.36, f32[2,4,64]{2,1,0:T(4,128)} %bitcast.37), custom_call_target="tpu_custom_call" | custom-call | tf_op jit(solution)/shard_map/token_gather/pallas_call | solution.py:138
  19.8 34.6 %expert_rows.1 = (f32[4,136,640]{2,1,0:T(8,128)}, f32[4,136,640]{2,1,0:T(8,128)}, f32[4,136,640]{2,1,0:T(8,128)}, f32[4,136,640]{2,1,0:T(8,128)}, bf16[16,640,3200]{2,1,0:T(8,128)(2,1)}, /*index=5*/s32[16]{0:T(128)}) custom-call(f32[8,8,128]{2,1,0:T(8,128)} %get-tuple-element.25.meta_ref, bf16[2,1024,640]{2,1,0:T(8,128)(2,1)} %bitcast.31, ...), custom_call_target="tpu_custom_call" | custom-call | flops 6000000000 | bytes 60000000 | tf_op jit(solution)/shard_map/expert_rows/pallas_call | solution.py:426
  54.5 0.0 copy-start.1
  54.5 1.1 %collective-permute-start.1 = (f32[4,136,640]{2,1,0:T(8,128)}, f32[4,136,640]{2,1,0:T(8,128)S(1)}, u32[]{:S(2)}, u32[]{:S(2)}) collective-permute-start(f32[4,136,640]{2,1,0:T(8,128)} %get-tuple-element.30), channel_id=1, source_target_pairs={{0,1},{1,0},{2,3},{3,2},{4,5},{5,4},{6,7},{7,6}} | collective-permute-start | bytes 4177928 | tf_op jit(solution)/shard_map/ppermute | solution.py:556
  55.5 0.0 collective-permute-start
  55.6 2.7 %collective-permute-done.1 = f32[4,136,640]{2,1,0:T(8,128)S(1)} collective-permute-done((f32[4,136,640]{2,1,0:T(8,128)}, f32[4,136,640]{2,1,0:T(8,128)S(1)}, u32[]{:S(2)}, u32[]{:S(2)}) %collective-permute-start.1) | collective-permute-done | bytes 1392672 | tf_op jit(solution)/shard_map/ppermute | solution.py:556
  58.3 1.2 %slice_add_fusion.1 = f32[2,128,640]{2,1,0:T(8,128)S(1)} fusion(f32[4,136,640]{2,1,0:T(8,128)S(1)} %collective-permute-done.1, f32[4,136,640]{2,1,0:T(8,128)} %get-tuple-element.29), kind=kLoop, calls=%fused_computation.1 | loop fusion | flops 163840 | bytes 1966080 | tf_op jit(solution)/shard_map/add | solution.py:566
  59.5 0.0 copy-start
  59.5 6.4 %collective-permute-start.3 = (f32[2,128,640]{2,1,0:T(8,128)S(1)}, f32[2,128,640]{2,1,0:T(8,128)S(1)}, u32[]{:S(2)}, u32[]{:S(2)}) collective-permute-start(f32[2,128,640]{2,1,0:T(8,128)S(1)} %slice_add_fusion.1), channel_id=1, source_target_pairs={{0,4},{4,0},{1,5},{5,1},{2,6},{6,2},{3,7},{7,3}} | collective-permute-start | bytes 1966088 | tf_op jit(solution)/shard_map/ppermute | solution.py:556
  65.9 0.0 copy-done.1
  65.9 0.1 slice_add_fusion
  66.0 0.4 collective-permute-start.2
  66.4 0.0 copy-done
  66.4 0.0 copy-start.2
  66.4 18.3 %weight_grads.2 = (f32[16,640,640]{2,1,0:T(8,128)}, f32[16,640,640]{2,1,0:T(8,128)}, f32[16,640,640]{2,1,0:T(8,128)}) custom-call(s32[16]{0:T(128)S(1)} %copy-done, bf16[16,640,3200]{2,1,0:T(8,128)(2,1)} %get-tuple-element.32.rows_hbm), custom_call_target="tpu_custom_call" | custom-call | flops 4000000000 | bytes 50000000 | tf_op jit(solution)/shard_map/weight_grads/pallas_call | solution.py:534
  84.8 0.0 collective-permute-done
  84.8 0.0 collective-permute-done.3
  84.8 0.0 copy-done.2
  84.8 0.1 fusion.5
  84.9 0.0 collective-permute-done.2
  84.9 0.1 fusion
  84.9 3.3 %collective-permute-start.4 = (f32[136,640]{1,0:T(8,128)S(1)}, f32[136,640]{1,0:T(8,128)S(1)}, u32[]{:S(2)}, u32[]{:S(2)}) collective-permute-start(f32[136,640]{1,0:T(8,128)S(1)} %fusion), channel_id=1, source_target_pairs={{0,4},{4,0},{1,5},{5,1},{2,6},{6,2},{3,7},{7,3}} | collective-permute-start | bytes 1044488 | tf_op jit(solution)/shard_map/ppermute | solution.py:556
  88.2 0.0 collective-permute-start.5
  88.2 12.1 %weight_grads.3 = (f32[16,640,640]{2,1,0:T(8,128)}, f32[16,640,640]{2,1,0:T(8,128)}, f32[16,640,640]{2,1,0:T(8,128)}) custom-call(s32[16]{0:T(128)S(1)} %copy-done, bf16[16,640,3200]{2,1,0:T(8,128)(2,1)} %get-tuple-element.32.rows_hbm, f32[16,640,640]{2,1,0:T(8,128)} %get-tuple-element.38.refs_0_, ...), custom_call_target="tpu_custom_call", output_to_operand_aliasing={{0}: (2, {}), {1}: (3, {}), {2}: (4, {})} | custom-call | flops 2400000000 | bytes 30000000 | tf_op jit(solution)/shard_map/weight_grads/pallas_call | solution.py:534
  100.4 0.0 collective-permute-done.4
  100.4 0.1 slice_bitcast_fusion.1
  100.5 0.6 maximum_bitcast_fusion
  101.1 0.0 collective-permute-done.5
  101.1 0.9 fusion.3
  (1 shorter events, 0.0 us)
Async XLA Ops:
  54.5 11.5 %copy-start.1 = (f32[4,136,640]{2,1,0:T(8,128)S(1)}, f32[4,136,640]{2,1,0:T(8,128)}, u32[]{:S(2)}) copy-start(f32[4,136,640]{2,1,0:T(8,128)} %get-tuple-element.29) | copy-start | bytes 4177924
  54.5 3.8 %collective-permute-start.1 = (f32[4,136,640]{2,1,0:T(8,128)}, f32[4,136,640]{2,1,0:T(8,128)S(1)}, u32[]{:S(2)}, u32[]{:S(2)}) collective-permute-start(f32[4,136,640]{2,1,0:T(8,128)} %get-tuple-element.30), channel_id=1, source_target_pairs={{0,1},{1,0},{2,3},{3,2},{4,5},{5,4},{6,7},{7,6}} | collective-permute-start | bytes 4177928 | tf_op jit(solution)/shard_map/ppermute | solution.py:556
  55.5 29.3 %collective-permute-start = (f32[4,136,640]{2,1,0:T(8,128)}, f32[4,136,640]{2,1,0:T(8,128)S(1)}, u32[]{:S(2)}, u32[]{:S(2)}) collective-permute-start(f32[4,136,640]{2,1,0:T(8,128)} %get-tuple-element.28), channel_id=1, source_target_pairs={{0,1},{1,0},{2,3},{3,2},{4,5},{5,4},{6,7},{7,6}} | collective-permute-start | bytes 4177928 | tf_op jit(solution)/shard_map/ppermute | solution.py:556
  59.5 7.0 %copy-start = (s32[16]{0:T(128)S(1)}, s32[16]{0:T(128)}, u32[]{:S(2)}) copy-start(s32[16]{0:T(128)} %get-tuple-element.31.cnt_ref) | copy-start | bytes 196
  59.5 25.3 %collective-permute-start.3 = (f32[2,128,640]{2,1,0:T(8,128)S(1)}, f32[2,128,640]{2,1,0:T(8,128)S(1)}, u32[]{:S(2)}, u32[]{:S(2)}) collective-permute-start(f32[2,128,640]{2,1,0:T(8,128)S(1)} %slice_add_fusion.1), channel_id=1, source_target_pairs={{0,4},{4,0},{1,5},{5,1},{2,6},{6,2},{3,7},{7,3}} | collective-permute-start | bytes 1966088 | tf_op jit(solution)/shard_map/ppermute | solution.py:556
  66.0 18.9 %collective-permute-start.2 = (f32[2,136,640]{2,1,0:T(8,128)S(1)}, f32[2,136,640]{2,1,0:T(8,128)S(1)}, u32[]{:S(2)}, u32[]{:S(2)}) collective-permute-start(f32[2,136,640]{2,1,0:T(8,128)S(1)} %slice_add_fusion), channel_id=1, source_target_pairs={{0,2},{2,0},{1,3},{3,1},{4,6},{6,4},{5,7},{7,5}} | collective-permute-start | bytes 2088968 | tf_op jit(solution)/shard_map/ppermute | solution.py:556
  66.4 18.4 %copy-start.2 = (f32[4,136,640]{2,1,0:T(8,128)S(1)}, f32[4,136,640]{2,1,0:T(8,128)}, u32[]{:S(2)}) copy-start(f32[4,136,640]{2,1,0:T(8,128)} %get-tuple-element.27) | copy-start | bytes 4177924
  84.9 15.4 %collective-permute-start.4 = (f32[136,640]{1,0:T(8,128)S(1)}, f32[136,640]{1,0:T(8,128)S(1)}, u32[]{:S(2)}, u32[]{:S(2)}) collective-permute-start(f32[136,640]{1,0:T(8,128)S(1)} %fusion), channel_id=1, source_target_pairs={{0,4},{4,0},{1,5},{5,1},{2,6},{6,2},{3,7},{7,3}} | collective-permute-start | bytes 1044488 | tf_op jit(solution)/shard_map/ppermute | solution.py:556
  88.2 12.8 %collective-permute-start.5 = (f32[128,640]{1,0:T(8,128)S(1)}, f32[128,640]{1,0:T(8,128)S(1)}, u32[]{:S(2)}, u32[]{:S(2)}) collective-permute-start(f32[128,640]{1,0:T(8,128)S(1)} %fusion.5), channel_id=1, source_target_pairs={{0,2},{2,0},{1,3},{3,1},{4,6},{6,4},{5,7},{7,5}} | collective-permute-start | bytes 983048 | tf_op jit(solution)/shard_map/ppermute | solution.py:556

commit v4 on v3

--- a/solution.py
+++ b/solution.py
@@ -18,7 +18,7 @@
 TOP_K = 4
 LOC = 16
 DIM = 640
-GATHER = 128
+GATHER = 256
 COMB = 256
 SMALL, BIG = 32, 256
 ROWS = 4640
@@ -241,7 +241,7 @@
         gcol[here, :] = jnp.zeros((GATHER, 1), F32)
         return carry
 
-    lax.fori_loop(0, 2 * n_comb, gather, 0)
+    lax.fori_loop(0, n_comb, gather, 0)
 
     def chunks(size, items, left=None, between=iter(())):
         lane = lax.broadcasted_iota(I32, (size, BLK), 1)
@@ -565,12 +565,12 @@
         y_in = swap(far_k[:2] + far_in[:2], "col")
         dx_in = swap(far_k[2:, :BLK] + far_in[2:, :BLK], "row")
         near_in = swap(near_s, "core")
-        early = weight_grads(0, 10, cnt, rows)
+        early = weight_grads(0, 9, cnt, rows)
         y_out = near_k[1] + near_in[1] + y_in[1]
         dx_out = near_k[3, :BLK] + near_in[3, :BLK] + dx_in[1]
         y_out, dx_out, early = lax.optimization_barrier((y_out, dx_out, early))
         y_far, dx_far = swap(y_out, "row"), swap(dx_out, "col")
-        g_gate, g_up, g_down = weight_grads(10, LOC, cnt, rows, early)
+        g_gate, g_up, g_down = weight_grads(9, LOC, cnt, rows, early)
         y = (near_k[0, :BLK] + near_in[0, :BLK] + y_in[0, :BLK] + y_far[:BLK]).astype(BF16).reshape(x.shape)
         dx = (near_k[2, :BLK] + near_in[2, :BLK] + dx_in[0] + dx_far).astype(BF16).reshape(x.shape)
         tail = slice(BLK, BLK + TOP_K)

time: 102 us -> 103 us (level)
  Pallas kernels: 84.2 us -> 90.7 us
  starting transfers between devices: 11.3 us -> 5.16 us
    ppermute x6, starting transfers between devices: 11.3 us -> 5.16 us  [swap(): return lax.ppermute(value, axis, [(0, 1), (1, 0)])]
    pallas_call x1, Pallas kernels: 34.6 us -> 39.9 us  [run_experts(): pl.pallas_call(expert_kernel, out_shape=(*[sums] * 4, jax.ShapeDtypeStruc...]
    pallas_call x2, Pallas kernels: 30.4 us -> 31.6 us  [weight_grads(): pl.pallas_call(functools.partial(wgrad_kernel, lo, hi, len(earlier)), out...]
  transfers between devices with their start and end apart: 6 -> 6, of which waited for: 1 -> 1; matrix products, arithmetic and copies ran while one was open for 2% -> 2% of each run, Pallas kernels for 30% -> 31%
where the time goes in v4:
time: 103 us; the launch traced here: 102 us
  Pallas kernels  90.7 us (88%)
  starting transfers between devices  5.16 us (5%)
  other arithmetic  2.83 us (3%)
  waiting for transfers between devices  2.76 us (3%)
    pallas_call x1, Pallas kernels, run_experts(): pl.pallas_call(expert_kernel, out_shape=(*[sums] * 4, jax.ShapeDtypeStruc...  39.9 us
    pallas_call x2, Pallas kernels, weight_grads(): pl.pallas_call(functools.partial(wgrad_kernel, lo, hi, len(earlier)), out...  31.6 us
    pallas_call x1, Pallas kernels, all_gather_tokens(): pl.pallas_call(gather_kernel, out_shape=(jax.ShapeDtypeStruct((2, N_DEV,...  19.2 us
    ppermute x6, starting transfers between devices, swap(): return lax.ppermute(value, axis, [(0, 1), (1, 0)])  5.16 us
    ppermute x6, waiting for transfers between devices, swap(): return lax.ppermute(value, axis, [(0, 1), (1, 0)])  2.76 us
  transfers between devices with their start and end apart: 6, of which 1 were waited for; matrix products, arithmetic and copies ran while one was open for 2% of the time, Pallas kernels for 31%

profile of v4, /device:TPU:0, one launch (start us, length us, event | category | flops | bytes accessed | tf_op | source)
XLA Modules:
  0.0 102.3 jit_solution(8512314114929963893)
XLA Ops:
  0.6 19.2 %token_gather.1 = (bf16[2,8,128,640]{3,2,1,0:T(8,128)(2,1)}, f32[8,8,128]{2,1,0:T(8,128)}) custom-call(bf16[128,640]{1,0:T(8,128)(2,1)} %bitcast.34, bf16[128,640]{1,0:T(8,128)(2,1)} %bitcast.35, s32[2,4,64]{2,1,0:T(4,128)} %bitcast.36, f32[2,4,64]{2,1,0:T(4,128)} %bitcast.37), custom_call_target="tpu_custom_call" | custom-call | tf_op jit(solution)/shard_map/token_gather/pallas_call | solution.py:138
  19.8 39.9 %expert_rows.1 = (f32[4,136,640]{2,1,0:T(8,128)}, f32[4,136,640]{2,1,0:T(8,128)}, f32[4,136,640]{2,1,0:T(8,128)}, f32[4,136,640]{2,1,0:T(8,128)}, bf16[16,640,3200]{2,1,0:T(8,128)(2,1)}, /*index=5*/s32[16]{0:T(128)}) custom-call(f32[8,8,128]{2,1,0:T(8,128)} %get-tuple-element.25.meta_ref, bf16[2,1024,640]{2,1,0:T(8,128)(2,1)} %bitcast.31, ...), custom_call_target="tpu_custom_call" | custom-call | flops 6000000000 | bytes 60000000 | tf_op jit(solution)/shard_map/expert_rows/pallas_call | solution.py:426
  59.7 0.0 copy-start.1
  59.8 1.0 %collective-permute-start.1 = (f32[4,136,640]{2,1,0:T(8,128)}, f32[4,136,640]{2,1,0:T(8,128)S(1)}, u32[]{:S(2)}, u32[]{:S(2)}) collective-permute-start(f32[4,136,640]{2,1,0:T(8,128)} %get-tuple-element.30), channel_id=1, source_target_pairs={{0,1},{1,0},{2,3},{3,2},{4,5},{5,4},{6,7},{7,6}} | collective-permute-start | bytes 4177928 | tf_op jit(solution)/shard_map/ppermute | solution.py:556
  60.8 0.0 collective-permute-start
  60.8 2.7 %collective-permute-done.1 = f32[4,136,640]{2,1,0:T(8,128)S(1)} collective-permute-done((f32[4,136,640]{2,1,0:T(8,128)}, f32[4,136,640]{2,1,0:T(8,128)S(1)}, u32[]{:S(2)}, u32[]{:S(2)}) %collective-permute-start.1) | collective-permute-done | bytes 1392672 | tf_op jit(solution)/shard_map/ppermute | solution.py:556
  63.6 1.2 %slice_add_fusion.1 = f32[2,128,640]{2,1,0:T(8,128)S(1)} fusion(f32[4,136,640]{2,1,0:T(8,128)S(1)} %collective-permute-done.1, f32[4,136,640]{2,1,0:T(8,128)} %get-tuple-element.29), kind=kLoop, calls=%fused_computation.1 | loop fusion | flops 163840 | bytes 1966080 | tf_op jit(solution)/shard_map/add | solution.py:566
  64.7 0.0 copy-start
  64.7 0.0 collective-permute-start.3
  64.8 0.0 copy-done.1
  64.8 0.1 slice_add_fusion
  64.9 2.0 %collective-permute-start.2 = (f32[2,136,640]{2,1,0:T(8,128)S(1)}, f32[2,136,640]{2,1,0:T(8,128)S(1)}, u32[]{:S(2)}, u32[]{:S(2)}) collective-permute-start(f32[2,136,640]{2,1,0:T(8,128)S(1)} %slice_add_fusion), channel_id=1, source_target_pairs={{0,2},{2,0},{1,3},{3,1},{4,6},{6,4},{5,7},{7,5}} | collective-permute-start | bytes 2088968 | tf_op jit(solution)/shard_map/ppermute | solution.py:556
  66.9 0.0 copy-done
  66.9 0.0 copy-start.2
  66.9 18.0 %weight_grads.2 = (f32[16,640,640]{2,1,0:T(8,128)}, f32[16,640,640]{2,1,0:T(8,128)}, f32[16,640,640]{2,1,0:T(8,128)}) custom-call(s32[16]{0:T(128)S(1)} %copy-done, bf16[16,640,3200]{2,1,0:T(8,128)(2,1)} %get-tuple-element.32.rows_hbm), custom_call_target="tpu_custom_call" | custom-call | flops 3600000000 | bytes 45000000 | tf_op jit(solution)/shard_map/weight_grads/pallas_call | solution.py:534
  84.9 0.0 collective-permute-done
  84.9 0.0 collective-permute-done.3
  84.9 0.0 copy-done.2
  84.9 0.1 fusion.5
  85.0 0.0 collective-permute-done.2
  85.0 0.1 fusion
  85.0 0.0 collective-permute-start.4
  85.1 2.0 %collective-permute-start.5 = (f32[128,640]{1,0:T(8,128)S(1)}, f32[128,640]{1,0:T(8,128)S(1)}, u32[]{:S(2)}, u32[]{:S(2)}) collective-permute-start(f32[128,640]{1,0:T(8,128)S(1)} %fusion.5), channel_id=1, source_target_pairs={{0,2},{2,0},{1,3},{3,1},{4,6},{6,4},{5,7},{7,5}} | collective-permute-start | bytes 983048 | tf_op jit(solution)/shard_map/ppermute | solution.py:556
  87.1 13.6 %weight_grads.3 = (f32[16,640,640]{2,1,0:T(8,128)}, f32[16,640,640]{2,1,0:T(8,128)}, f32[16,640,640]{2,1,0:T(8,128)}) custom-call(s32[16]{0:T(128)S(1)} %copy-done, bf16[16,640,3200]{2,1,0:T(8,128)(2,1)} %get-tuple-element.32.rows_hbm, f32[16,640,640]{2,1,0:T(8,128)} %get-tuple-element.38.refs_0_, ...), custom_call_target="tpu_custom_call", output_to_operand_aliasing={{0}: (2, {}), {1}: (3, {}), {2}: (4, {})} | custom-call | flops 2800000000 | bytes 35000000 | tf_op jit(solution)/shard_map/weight_grads/pallas_call | solution.py:534
  100.7 0.0 collective-permute-done.4
  100.7 0.1 slice_bitcast_fusion.1
  100.8 0.6 maximum_bitcast_fusion
  101.4 0.0 collective-permute-done.5
  101.4 0.9 fusion.3
  (1 shorter events, 0.0 us)
Async XLA Ops:
  59.7 5.0 %copy-start.1 = (f32[4,136,640]{2,1,0:T(8,128)S(1)}, f32[4,136,640]{2,1,0:T(8,128)}, u32[]{:S(2)}) copy-start(f32[4,136,640]{2,1,0:T(8,128)} %get-tuple-element.29) | copy-start | bytes 4177924
  59.8 3.8 %collective-permute-start.1 = (f32[4,136,640]{2,1,0:T(8,128)}, f32[4,136,640]{2,1,0:T(8,128)S(1)}, u32[]{:S(2)}, u32[]{:S(2)}) collective-permute-start(f32[4,136,640]{2,1,0:T(8,128)} %get-tuple-element.30), channel_id=1, source_target_pairs={{0,1},{1,0},{2,3},{3,2},{4,5},{5,4},{6,7},{7,6}} | collective-permute-start | bytes 4177928 | tf_op jit(solution)/shard_map/ppermute | solution.py:556
  60.8 24.1 %collective-permute-start = (f32[4,136,640]{2,1,0:T(8,128)}, f32[4,136,640]{2,1,0:T(8,128)S(1)}, u32[]{:S(2)}, u32[]{:S(2)}) collective-permute-start(f32[4,136,640]{2,1,0:T(8,128)} %get-tuple-element.28), channel_id=1, source_target_pairs={{0,1},{1,0},{2,3},{3,2},{4,5},{5,4},{6,7},{7,6}} | collective-permute-start | bytes 4177928 | tf_op jit(solution)/shard_map/ppermute | solution.py:556
  64.7 2.1 %copy-start = (s32[16]{0:T(128)S(1)}, s32[16]{0:T(128)}, u32[]{:S(2)}) copy-start(s32[16]{0:T(128)} %get-tuple-element.31.cnt_ref) | copy-start | bytes 196
  64.7 20.1 %collective-permute-start.3 = (f32[2,128,640]{2,1,0:T(8,128)S(1)}, f32[2,128,640]{2,1,0:T(8,128)S(1)}, u32[]{:S(2)}, u32[]{:S(2)}) collective-permute-start(f32[2,128,640]{2,1,0:T(8,128)S(1)} %slice_add_fusion.1), channel_id=1, source_target_pairs={{0,4},{4,0},{1,5},{5,1},{2,6},{6,2},{3,7},{7,3}} | collective-permute-start | bytes 1966088 | tf_op jit(solution)/shard_map/ppermute | solution.py:556
  64.9 20.1 %collective-permute-start.2 = (f32[2,136,640]{2,1,0:T(8,128)S(1)}, f32[2,136,640]{2,1,0:T(8,128)S(1)}, u32[]{:S(2)}, u32[]{:S(2)}) collective-permute-start(f32[2,136,640]{2,1,0:T(8,128)S(1)} %slice_add_fusion), channel_id=1, source_target_pairs={{0,2},{2,0},{1,3},{3,1},{4,6},{6,4},{5,7},{7,5}} | collective-permute-start | bytes 2088968 | tf_op jit(solution)/shard_map/ppermute | solution.py:556
  66.9 18.0 %copy-start.2 = (f32[4,136,640]{2,1,0:T(8,128)S(1)}, f32[4,136,640]{2,1,0:T(8,128)}, u32[]{:S(2)}) copy-start(f32[4,136,640]{2,1,0:T(8,128)} %get-tuple-element.27) | copy-start | bytes 4177924
  85.0 15.7 %collective-permute-start.4 = (f32[136,640]{1,0:T(8,128)S(1)}, f32[136,640]{1,0:T(8,128)S(1)}, u32[]{:S(2)}, u32[]{:S(2)}) collective-permute-start(f32[136,640]{1,0:T(8,128)S(1)} %fusion), channel_id=1, source_target_pairs={{0,4},{4,0},{1,5},{5,1},{2,6},{6,2},{3,7},{7,3}} | collective-permute-start | bytes 1044488 | tf_op jit(solution)/shard_map/ppermute | solution.py:556
  85.1 16.3 %collective-permute-start.5 = (f32[128,640]{1,0:T(8,128)S(1)}, f32[128,640]{1,0:T(8,128)S(1)}, u32[]{:S(2)}, u32[]{:S(2)}) collective-permute-start(f32[128,640]{1,0:T(8,128)S(1)} %fusion.5), channel_id=1, source_target_pairs={{0,2},{2,0},{1,3},{3,1},{4,6},{6,4},{5,7},{7,5}} | collective-permute-start | bytes 983048 | tf_op jit(solution)/shard_map/ppermute | solution.py:556
